TPU v7x, 512 devices: a whole 4x4x16 slice. The times are simulated.
512 devices in a mesh: img: 32 (over y_hi, z), sp: 16 (over y_lo, x, core).
Axes of the slice: x: 4, y: 4 (y_hi: 2, y_lo: 2; y = y_hi * 2 + y_lo), z: 16, core: 2. Of those that a mesh axis runs over, the one named last changes fastest.
Arguments:
- patches: bfloat16 [65536, 1280], P(('img', 'sp')), parts along dimension 0, may hold values from -6 to 6
- pos_ids: int32 [2, 65536], P(None, 'img'), parts along dimension 1, may hold values from 0 to 127, as said below
- norm_gain: float32 [1280], replicated, may hold values from 0.5 to 1.5
- norm_bias: float32 [1280], replicated, may hold values from -3 to 3
- qkv_weight: bfloat16 [1280, 3, 1280], P(None, None, 'sp')
- qkv_bias: float32 [3, 1280], replicated, may hold values from -3 to 3
- proj_weight: bfloat16 [1280, 1280], P('sp'), may hold values from -0.15625 to 0.15625
- proj_bias: float32 [1280], replicated, may hold values from -3 to 3
- merge_gain: float32 [1280], replicated, may hold values from 0.5 to 1.5
- merge_bias: float32 [1280], replicated, may hold values from -3 to 3
- fc1_weight: bfloat16 [5120, 5120], P(None, 'sp'), may hold values from -0.078125 to 0.078125
- fc1_bias: float32 [5120], P('sp'), may hold values from -3 to 3
Outputs:
- vit_out: bfloat16 [65536, 1280], P(('img', 'sp')), parts along dimension 0
- merged_hidden: bfloat16 [16384, 5120], P('img', 'sp'), parts along dimension 0
There are 32 independent parts, one for each index of `img`. A program takes and returns all parts, laid end to end along the dimension named above; an argument that names none is the same for every part. Nothing has to cross between parts.
Inputs may be any that keep to these rules, and one draw needn't show every extreme that they name: pos_ids[0] and pos_ids[1] are the row and column of each patch on a grid of 2 R by 2 C patches, where the grid of 2x2 blocks has R rows and C columns, R C = 512, and one of R and C equals min(8, 512); each aligned run of 4 patches is one 2x2 block in row-major order inside it; every block of the grid appears once, in the order that the argument gives.
All inputs are finite; a program needn't handle non-finite values.
Results may differ from a plain program's by a relative error of at most 0.006.
Values may be sent and summed in bfloat16 or wider, within the bound.
A program may use at most 64 MiB of HBM per device.

v0:
```python
import jax
import jax.numpy as jnp
from jax import lax
from jax.sharding import PartitionSpec as P

HEADS = 16


def layer_norm(values, gain, bias):
    mean = jnp.mean(values, axis=-1, keepdims=True)
    centered = values - mean
    var = jnp.mean(centered * centered, axis=-1, keepdims=True)
    return centered * lax.rsqrt(var + 1e-06) * gain + bias


def rotate(values, positions, nheads):
    count = values.shape[0]
    hdim = values.shape[1] // nheads
    quarter = hdim // 4
    inv = 1.0 / 10000.0 ** (jnp.arange(quarter, dtype=jnp.float32) * 2.0 / (hdim // 2))
    rows = positions[0].astype(jnp.float32)[:, None] * inv
    cols = positions[1].astype(jnp.float32)[:, None] * inv
    angle = jnp.concatenate([rows, cols, rows, cols], axis=1)
    cosine = jnp.cos(angle)[:, None, :]
    sine = jnp.sin(angle)[:, None, :]
    shaped = values.reshape(count, nheads, hdim)
    half = hdim // 2
    turned = jnp.concatenate([-shaped[..., half:], shaped[..., :half]], axis=-1)
    return (shaped * cosine + turned * sine).reshape(count, nheads * hdim)


def attend(query, keys, value, nheads, hdim):
    count = query.shape[0]
    block = min(512, count)
    qblocks = query.reshape(count // block, block, nheads, hdim)
    kshaped = keys.reshape(count, nheads, hdim)
    vshaped = value.reshape(count, nheads, hdim)
    scale = 1.0 / jnp.sqrt(jnp.float32(hdim))

    def one_block(qpart):
        scores = (
            jnp.einsum("bhd,khd->hbk", qpart, kshaped, preferred_element_type=jnp.float32) * scale
        )
        top = jnp.max(scores, axis=-1, keepdims=True)
        expo = jnp.exp(scores - top)
        weights = (expo / jnp.sum(expo, axis=-1, keepdims=True)).astype(jnp.bfloat16)
        result = jnp.einsum("hbk,khd->bhd", weights, vshaped, preferred_element_type=jnp.float32)
        return result.astype(jnp.bfloat16).reshape(block, nheads * hdim)

    return lax.map(one_block, qblocks).reshape(count, nheads * hdim)


def per_device(
    patches,
    pos_ids,
    norm_gain,
    norm_bias,
    qkv_weight,
    qkv_bias,
    proj_weight,
    proj_bias,
    merge_gain,
    merge_bias,
    fc1_weight,
    fc1_bias,
):
    groups = lax.axis_size("sp")
    where = lax.axis_index("sp")
    prow = patches.shape[0]
    width = patches.shape[1]
    heads_local = HEADS // groups
    hdim = width // HEADS
    local_width = width // groups
    xfloat = patches.astype(jnp.float32)
    normed = layer_norm(xfloat, norm_gain, norm_bias).astype(jnp.bfloat16)
    bias_local = lax.dynamic_slice_in_dim(qkv_bias, where * local_width, local_width, 1)
    qkv = (
        jnp.einsum(
            "pd,dcn->pcn",
            lax.all_gather(normed, "sp", axis=0, tiled=True),
            qkv_weight,
            preferred_element_type=jnp.float32,
        )
        + bias_local[None]
    )
    query = rotate(qkv[:, 0], pos_ids, heads_local).astype(jnp.bfloat16)
    keys = rotate(qkv[:, 1], pos_ids, heads_local).astype(jnp.bfloat16)
    value = qkv[:, 2].astype(jnp.bfloat16)
    spread = jnp.stack([query, keys, value])
    attended = attend(spread[0], spread[1], spread[2], heads_local, hdim)
    returned = lax.all_to_all(attended, "sp", split_axis=0, concat_axis=1, tiled=True)
    projected = jnp.dot(
        returned,
        lax.all_gather(proj_weight, "sp", axis=0, tiled=True),
        preferred_element_type=jnp.float32,
    )
    vit_out = (xfloat + projected + proj_bias).astype(jnp.bfloat16)
    zn = layer_norm(vit_out.astype(jnp.float32), merge_gain, merge_bias).astype(jnp.bfloat16)
    blocks = zn.reshape(prow // 4, 4 * width)
    hidden = (
        jnp.dot(
            lax.all_gather(blocks, "sp", axis=0, tiled=True),
            fc1_weight,
            preferred_element_type=jnp.float32,
        )
        + fc1_bias
    )
    merged_hidden = jax.nn.gelu(hidden, approximate=False).astype(jnp.bfloat16)
    return (vit_out, merged_hidden)


def solution(mesh):
    return jax.shard_map(
        per_device,
        mesh=mesh,
        in_specs=(
            P(("img", "sp"), None),
            P(None, "img"),
            P(),
            P(),
            P(None, None, "sp"),
            P(),
            P("sp", None),
            P(),
            P(),
            P(),
            P(None, "sp"),
            P("sp"),
        ),
        out_specs=(P(("img", "sp"), None), P("img", "sp")),
        check_vma=False,
    )
```

profile of v0, /device:TPU:1, one launch (start us, length us, event | category | flops | bytes accessed | tf_op | source)
XLA Modules:
  0.0 179.0 jit_solution(13531973200545113736)
XLA Ops:
  7.2 1.2 convert_reduce_fusion
  8.5 1.2 fusion.18
  9.7 2.0 %fusion.21 = bf16[128,1280]{1,0:T(8,128)(2,1)} fusion(bf16[128,1280]{1,0:T(8,128)(2,1)} %param.14, f32[1280]{0:T(1024)} %param.17, f32[1280]{0:T(1024)} %param.16, f32[128]{0:T(128)S(1)} %add_rsqrt_fusion.1, f32[128]{0:T(128)S(1)} %broadcast_multiply_fusion.1), kind=kLoop, calls=%fused_computation.32 | loop fusion | flops 983040 | bytes 666624 | tf_op jit(solution)/shard_map/convert_element_type | solution.py:75
  12.5 0.8 slice_convert_fusion.2
  13.3 0.8 constant_dynamic-slice_fusion
  14.1 0.8 multiply_bitcast_fusion.1
  14.8 49.5 %all-gather.4.cloned.1.call-done = bf16[2048,1280]{1,0:T(8,128)(2,1)} async-done(((bf16[128,1280]{1,0:T(8,128)(2,1)}), bf16[2048,1280]{1,0:T(8,128)(2,1)}) %all-gather.4.cloned.1.call-update) | async-done | bytes 5242896 | tf_op jit(solution)/shard_map/all_gather | solution.py:80
  64.4 4.2 %fusion.42 = f32[2048,240]{0,1:S(1)} fusion(bf16[2048,1280]{1,0:T(8,128)(2,1)} %all-gather.4.cloned.1.call-done, bf16[1280,240]{0,1:T(8,128)(2,1)} %bitcast.59), kind=kOutput, calls=%fused_computation.80 | convolution fusion | flops 1258291200 | bytes 7823360
  69.7 3.2 %fusion.30 = (bf16[2048,1,80]{0,2,1:T(8,128)(2,1)}, bf16[2048,1,80]{0,2,1:T(8,128)(2,1)S(1)}) fusion(f32[2048,3,80]{0,2,1:T(8,128)S(1)} %broadcast_add_fusion, f32[2048,1,40]{0,2,1:T(8,128)S(1)} %get-tuple-element.60, f32[2048,1,40]{0,2,1:T(8,128)S(1)} %get-tuple-element.59, f32[2048,1,20]{0,2,1:T(8,128)S(1)} %copy-done.2, ...), kind=kLoop, calls=%fused_computation.43 | loop fusion | flops 2129920 | bytes 3604480 | tf_op jit(solution)/shard_map/convert_element_type | solution.py:87
  73.6 17.8 %while.10 = (s32[]{:T(128)}, bf16[4,512,80]{1,2,0:T(8,128)(2,1)}, bf16[4,512,1,80]{1,3,2,0:T(8,128)(2,1)}, bf16[2048,1,80]{0,2,1:T(8,128)(2,1)}, bf16[2048,1,80]{0,2,1:T(8,128)(2,1)}, /*index=5*/s32[]{:T(128)}) while((s32[]{:T(128)}, bf16[4,512,80]{1,2,0:T(8,128)(2,1)}, bf16[4,512,1,80]{1,3,2,0:T(8,128)(2,1)}, bf16[2048,1,80]{0,2,1:T(8,128)(2,1)}, ...), condition=%wide.region_5.6_spmd, body=%wide.region_2.5_spmd.sunk | while | flops 345021440 | bytes 14724193 | solution.py:50
  73.6 1.9 %multiply_reduce_fusion.2 = (f32[512]{0:T(512)S(1)}, f32[512,2048]{1,0:T(8,128)S(1)}) fusion(bf16[2048,1,80]{0,2,1:T(8,128)(2,1)} %get-tuple-element.119, bf16[4,512,1,80]{1,3,2,0:T(8,128)(2,1)} %get-tuple-element.118, s32[]{:T(128)} %get-tuple-element.110), kind=kOutput, calls=%fused_computation.2.clone.1 | convolution fusion | flops 169868800 | bytes 4606464 | tf_op jit(solution)/shard_map/while/body/eval_jaxpr/bhd,khd->hbk/dot_general | solution.py:42
  75.5 0.8 fusion.53
  76.3 1.7 fusion.54
  78.1 1.9 %multiply_reduce_fusion.2 = (f32[512]{0:T(512)S(1)}, f32[512,2048]{1,0:T(8,128)S(1)}) fusion(bf16[2048,1,80]{0,2,1:T(8,128)(2,1)} %get-tuple-element.119, bf16[4,512,1,80]{1,3,2,0:T(8,128)(2,1)} %get-tuple-element.118, s32[]{:T(128)} %get-tuple-element.110), kind=kOutput, calls=%fused_computation.2.clone.1 | convolution fusion | flops 169868800 | bytes 4606464 | tf_op jit(solution)/shard_map/while/body/eval_jaxpr/bhd,khd->hbk/dot_general | solution.py:42
  79.9 0.8 fusion.53
  80.8 1.7 fusion.54
  82.5 1.9 %multiply_reduce_fusion.2 = (f32[512]{0:T(512)S(1)}, f32[512,2048]{1,0:T(8,128)S(1)}) fusion(bf16[2048,1,80]{0,2,1:T(8,128)(2,1)} %get-tuple-element.119, bf16[4,512,1,80]{1,3,2,0:T(8,128)(2,1)} %get-tuple-element.118, s32[]{:T(128)} %get-tuple-element.110), kind=kOutput, calls=%fused_computation.2.clone.1 | convolution fusion | flops 169868800 | bytes 4606464 | tf_op jit(solution)/shard_map/while/body/eval_jaxpr/bhd,khd->hbk/dot_general | solution.py:42
  84.4 0.8 fusion.53
  85.2 1.7 fusion.54
  86.9 1.9 %multiply_reduce_fusion.2 = (f32[512]{0:T(512)S(1)}, f32[512,2048]{1,0:T(8,128)S(1)}) fusion(bf16[2048,1,80]{0,2,1:T(8,128)(2,1)} %get-tuple-element.119, bf16[4,512,1,80]{1,3,2,0:T(8,128)(2,1)} %get-tuple-element.118, s32[]{:T(128)} %get-tuple-element.110), kind=kOutput, calls=%fused_computation.2.clone.1 | convolution fusion | flops 169868800 | bytes 4606464 | tf_op jit(solution)/shard_map/while/body/eval_jaxpr/bhd,khd->hbk/dot_general | solution.py:42
  88.8 0.8 fusion.53
  89.7 1.7 fusion.54
  91.4 2.0 %copy.21 = bf16[4,512,80]{1,0,2:T(4,128)(2,1)} copy(bf16[4,512,80]{1,2,0:T(8,128)(2,1)} %get-tuple-element.29) | data formatting | bytes 655360 | tf_op jit(solution)/shard_map/while | solution.py:50
  93.4 1.8 %all_to_all.14 = bf16[16,128,80]{1,0,2:T(8,128)(2,1)} reshape(bf16[4,512,80]{1,0,2:T(4,128)(2,1)} %copy.21) | data formatting | bytes 655360 | tf_op jit(solution)/shard_map/all_to_all | solution.py:91
  95.2 1.8 copy.22
  97.0 4.2 %all-to-all-start = ((bf16[16,128,80]{1,2,0:T(8,128)(2,1)}), bf16[16,128,80]{1,2,0:T(8,128)(2,1)}, u32[]{:S(2)}, u32[]{:S(2)}) async-start(bf16[16,128,80]{1,2,0:T(8,128)(2,1)} %copy.22), calls=%async_computation | async-start | bytes 655360 | tf_op jit(solution)/shard_map/all_to_all | solution.py:91
  101.3 10.4 %all-gather.6.cloned.1.call-done = bf16[1280,1280]{1,0:T(8,128)(2,1)} async-done(((bf16[80,1280]{1,0:T(8,128)(2,1)}), bf16[1280,1280]{1,0:T(8,128)(2,1)}) %all-gather.6.cloned.1.call-update) | async-done | bytes 3276816 | tf_op jit(solution)/shard_map/all_gather | solution.py:94
  111.7 2.8 %convert_reduce_fusion.1 = (f32[128]{0:T(128)S(1)}, bf16[128,1280]{1,0:T(8,128)(2,1)S(1)}) fusion(f32[1280]{0:T(1024)S(1)} %copy-done.4, bf16[128,1280]{0,1:T(8,128)(2,1)} %bitcast.14, bf16[1280,1280]{1,0:T(8,128)(2,1)} %all-gather.6.cloned.1.call-done, bf16[128,1280]{1,0:T(8,128)(2,1)} %param.14), kind=kOutput, calls=%fused_computation.24 | convolution fusion | flops 420413312 | bytes 4265472 | tf_op jit(solution)/shard_map/dot_general | solution.py:92
  115.2 1.0 fusion.25
  116.2 1.9 %reshape.408 = bf16[32,5120]{1,0:T(8,128)(2,1)} reshape(bf16[128,1280]{1,0:T(8,128)(2,1)} %fusion.25) | data formatting | bytes 655360 | tf_op jit(solution)/shard_map/reshape | solution.py:99
  118.2 47.9 %all-gather.8.cloned.1.call-done = bf16[512,5120]{1,0:T(8,128)(2,1)} async-done(((bf16[32,5120]{1,0:T(8,128)(2,1)}), bf16[512,5120]{1,0:T(8,128)(2,1)}) %all-gather.8.cloned.1.call-update) | async-done | bytes 5242896 | tf_op jit(solution)/shard_map/all_gather | solution.py:102
  166.0 6.4 %fusion.28 = bf16[512,320]{0,1:T(8,128)(2,1)} fusion(bf16[512,5120]{1,0:T(8,128)(2,1)} %all-gather.8.cloned.1.call-done, bf16[5120,320]{0,1:T(8,128)(2,1)S(1)} %copy-done, f32[320]{0:T(512)S(1)} %copy-done.7), kind=kOutput, calls=%fused_computation.39 | convolution fusion | flops 1688535040 | bytes 8848640 | tf_op jit(solution)/shard_map/dot_general | solution.py:101
  (40 shorter events, 3.5 us)
Async XLA Ops:
  7.2 158.9 %copy-start = (bf16[5120,320]{0,1:T(8,128)(2,1)S(1)}, bf16[5120,320]{0,1:T(8,128)(2,1)}, u32[]{:S(2)}) copy-start(bf16[5120,320]{0,1:T(8,128)(2,1)} %param.24) | copy-start | bytes 9830404
  7.2 57.2 %all-gather.4.cloned.1.call-start = ((), (), s32[]{:S(2)}) async-start(), calls=%async_computation.1 | async-start | bytes 5570560 | tf_op jit(solution)/shard_map/all_gather | solution.py:80
  11.7 100.0 %all-gather.6.cloned.1.call-start = ((), (), s32[]{:S(2)}) async-start(), calls=%async_computation.2 | async-start | bytes 3481600 | tf_op jit(solution)/shard_map/all_gather | solution.py:94
  68.5 1.1 copy-start.2
  73.6 38.1 %copy-start.4 = (f32[1280]{0:T(1024)S(1)}, f32[1280]{0:T(1024)}, u32[]{:S(2)}) copy-start(f32[1280]{0:T(1024)} %param.21) | copy-start | bytes 15364
  73.6 2.7 %copy-start.3 = (bf16[2048,1,80]{0,2,1:T(8,128)(2,1)S(1)}, bf16[2048,1,80]{0,2,1:T(8,128)(2,1)}, u32[]{:S(2)}) copy-start(bf16[2048,1,80]{0,2,1:T(8,128)(2,1)} %get-tuple-element.120) | copy-start | bytes 983044 | tf_op jit(solution)/shard_map/while
  78.1 2.7 %copy-start.3 = (bf16[2048,1,80]{0,2,1:T(8,128)(2,1)S(1)}, bf16[2048,1,80]{0,2,1:T(8,128)(2,1)}, u32[]{:S(2)}) copy-start(bf16[2048,1,80]{0,2,1:T(8,128)(2,1)} %get-tuple-element.120) | copy-start | bytes 983044 | tf_op jit(solution)/shard_map/while
  82.5 2.7 %copy-start.3 = (bf16[2048,1,80]{0,2,1:T(8,128)(2,1)S(1)}, bf16[2048,1,80]{0,2,1:T(8,128)(2,1)}, u32[]{:S(2)}) copy-start(bf16[2048,1,80]{0,2,1:T(8,128)(2,1)} %get-tuple-element.120) | copy-start | bytes 983044 | tf_op jit(solution)/shard_map/while
  86.9 2.7 %copy-start.3 = (bf16[2048,1,80]{0,2,1:T(8,128)(2,1)S(1)}, bf16[2048,1,80]{0,2,1:T(8,128)(2,1)}, u32[]{:S(2)}) copy-start(bf16[2048,1,80]{0,2,1:T(8,128)(2,1)} %get-tuple-element.120) | copy-start | bytes 983044 | tf_op jit(solution)/shard_map/while
  91.4 23.8 %copy-start.5 = (f32[1280]{0:T(1024)S(1)}, f32[1280]{0:T(1024)}, u32[]{:S(2)}) copy-start(f32[1280]{0:T(1024)} %param.23) | copy-start | bytes 15364
  91.4 23.8 %copy-start.6 = (f32[1280]{0:T(1024)S(1)}, f32[1280]{0:T(1024)}, u32[]{:S(2)}) copy-start(f32[1280]{0:T(1024)} %param.22) | copy-start | bytes 15364
  93.4 72.6 %copy-start.7 = (f32[320]{0:T(512)S(1)}, f32[320]{0:T(512)}, u32[]{:S(2)}) copy-start(f32[320]{0:T(512)} %param.25) | copy-start | bytes 3844
  97.0 14.7 %all-to-all-start = ((bf16[16,128,80]{1,2,0:T(8,128)(2,1)}), bf16[16,128,80]{1,2,0:T(8,128)(2,1)}, u32[]{:S(2)}, u32[]{:S(2)}) async-start(bf16[16,128,80]{1,2,0:T(8,128)(2,1)} %copy.22), calls=%async_computation | async-start | bytes 655360 | tf_op jit(solution)/shard_map/all_to_all | solution.py:91
  101.2 64.8 %all-gather.8.cloned.1.call-start = ((), (), s32[]{:S(2)}) async-start(), calls=%async_computation.3 | async-start | bytes 5570560 | tf_op jit(solution)/shard_map/all_gather | solution.py:102
  114.5 0.7 copy-start.1
Sparse Core Ops, SparseCore 0:
  11.8 52.4 all-gather.3
  66.5 45.1 all-gather.5
  118.3 47.7 all-gather.7
where the time goes:
time: 180 us; the launch traced here: 179 us
  waiting for transfers between devices  109 us (61%)
  matrix products  27.9 us (16%)
  other arithmetic  14.1 us (8%)
  between operations  13.8 us (8%)
  local copies, waits for them, and re-layouts  10.3 us (6%)
  starting transfers between devices  4.34 us (2%)
    all_gather x1, waiting for transfers between devices, per_device(): lax.all_gather(normed, 'sp', axis=0, tiled=True)  49.5 us
    all_gather x1, waiting for transfers between devices, per_device(): lax.all_gather(blocks, 'sp', axis=0, tiled=True)  47.9 us
    all_gather x1, waiting for transfers between devices, per_device(): lax.all_gather(proj_weight, 'sp', axis=0, tiled=True)  10.4 us
    dot_general x4, matrix products, one_block(): jnp.einsum('bhd,khd->hbk', qpart, kshaped, preferred_element_type=jnp.flo...  7.49 us
    dot_general x4, matrix products, one_block(): jnp.einsum('hbk,khd->bhd', weights, vshaped, preferred_element_type=jnp.f...  6.99 us
    dot_general x1, matrix products, per_device(): jnp.dot(lax.all_gather(blocks, 'sp', axis=0, tiled=True), fc1_weight, pre...  6.44 us
    all_to_all x1, starting transfers between devices, per_device(): lax.all_to_all(attended, 'sp', split_axis=0, concat_axis=1, tiled=True)  4.22 us
    unnamed x1, matrix products  4.17 us
  transfers between devices with their start and end apart: 4, of which 3 were waited for; matrix products, arithmetic and copies ran while one was open for 18% of the time, Pallas kernels for 0%

commit v1 on v0

v1 whole, which is shorter than its diff:
```python
import math

import jax
import jax.numpy as jnp
from jax import lax
from jax.experimental import pallas as pl
from jax.experimental.pallas import tpu as pltpu
from jax.sharding import PartitionSpec as P

MESH = pl.DeviceIdType.MESH
HEADS = 16
D = 1280
HDIM = 80
PATCHES = 2048
HIDDEN = 5120
SHARE = 320
ROLES = 8
W_CUT = ((0, 48), (48, 32))
SCALE = math.log2(math.e) / math.sqrt(HDIM)


def norm_rows(v, gain, bias):
    mean = jnp.mean(v, axis=-1, keepdims=True)
    cen = v - mean
    var = jnp.mean(cen * cen, axis=-1, keepdims=True)
    return cen * lax.rsqrt(var + 1e-06) * gain + bias


def kernel(
    x_ref, pos_ref, g1_ref, b1_ref, wq_hbm, bq_ref, wp_hbm, pb_ref, g2_ref, b2_ref, fc_hbm, fb_ref,
    vit_hbm, hid_hbm,
    gat, blk, wg, att, osend, qt, kk, vt, sc, fcv, wqv, bcol, fcol, zf, vitv, hidv,
    send, recv, asend, arecv, local,
):
    me = lax.axis_index("sp")
    core = me % 2
    mx = (me // 2) % 4
    my = me // 8

    def dev(dx, dy, p):
        return ((my + dy) % 2) * 8 + ((mx + dx) % 4) * 2 + (core + p) % 2

    wq_copy = pltpu.make_async_copy(wq_hbm, wqv, local.at[0])
    wp_copy = pltpu.make_async_copy(wp_hbm, wg.at[0, 0], local.at[1])
    fc_copy = pltpu.make_async_copy(fc_hbm, fcv, local.at[2])
    wq_copy.start()
    wp_copy.start()
    fc_copy.start()

    xf = x_ref[...].astype(jnp.float32)
    normed = norm_rows(xf, g1_ref[...].reshape(1, D), b1_ref[...].reshape(1, D)).astype(jnp.bfloat16)
    gat[0, 0] = normed.reshape(2, 64, D)

    barrier = pltpu.get_barrier_semaphore()
    for step in range(1, 16):
        pl.semaphore_signal(barrier, inc=1, device_id={"sp": (me + step) % 16}, device_id_type=MESH)
    pl.semaphore_wait(barrier, 15)

    class Gather:
        def __init__(self, index, piece):
            self.index, self.piece, self.sends = index, piece, []

        def put(self, src, dst, dx, dy, p):
            copy = pltpu.make_async_remote_copy(
                src_ref=self.piece(*src),
                dst_ref=self.piece(*dst),
                send_sem=send.at[self.index, len(self.sends)],
                recv_sem=recv.at[self.index, *dst],
                device_id={"sp": dev(dx, dy, p)},
                device_id_type=MESH,
            )
            copy.start()
            self.sends.append(copy)

        def pass_on(self, r, h, dx, dy):
            role = 4 * ((r // 4 + dy) % 2) + (r % 4 - dx) % 4
            self.put((r, 0, h), (role, 0, h), dx, dy, 0)

        def share(self, r, h):
            self.put((r, 0, h), (r, 1, h), 0, 0, 1)

        def wait(self, r, p, h):
            pltpu.make_async_remote_copy(
                src_ref=self.piece(r, p, h),
                dst_ref=self.piece(r, p, h),
                send_sem=send.at[self.index, 0],
                recv_sem=recv.at[self.index, r, p, h],
                device_id={"sp": dev(0, 0, 1)},
                device_id_type=MESH,
            ).wait_recv()

        def wait_partner(self, roles):
            for r in roles:
                for h in range(2):
                    self.wait(r, 1, h)

        def begin(self):
            for h in range(2):
                self.pass_on(0, h, 1, 0)
                self.pass_on(0, 1 - h, -1, 0)
                self.pass_on(0, h, 0, 1)
            for h in range(2):
                self.share(0, h)

        def first(self):
            self.wait(3, 0, 0)
            self.pass_on(3, 0, 1, 0)
            self.wait(1, 0, 1)
            self.pass_on(1, 1, -1, 0)
            self.wait(4, 0, 0)
            self.pass_on(4, 0, 1, 0)
            self.pass_on(4, 0, -1, 0)
            self.share(3, 0)
            self.share(1, 1)
            self.share(4, 0)
            self.wait(4, 0, 1)
            self.pass_on(4, 1, 1, 0)
            self.pass_on(4, 1, -1, 0)
            self.wait(3, 0, 1)
            self.wait(1, 0, 0)
            self.share(4, 1)
            self.share(3, 1)
            self.share(1, 0)

        def second(self):
            for h in range(2):
                self.wait(2, 0, h)
                self.pass_on(2, h, 0, 1)
                self.share(2, h)

        def third(self, h):
            for r in (5, 7, 6):
                self.wait(r, 0, h)
                self.share(r, h)

        def drain(self):
            for copy in self.sends:
                copy.wait_send()

    g1 = Gather(0, lambda r, p, h: gat.at[r, p, h])
    gw = Gather(1, lambda r, p, h: wg.at[r, p, pl.ds(*W_CUT[h])])
    g2 = Gather(2, lambda r, p, h: blk.at[r, p, h])

    g1.begin()

    lane = lax.broadcasted_iota(jnp.int32, (HDIM, D), 1)
    sub = lax.broadcasted_iota(jnp.int32, (HDIM, D), 0)
    mine = lane == sub + me * HDIM
    for c in range(3):
        col = jnp.sum(jnp.where(mine, bq_ref[c : c + 1, :], 0.0), axis=1, keepdims=True)
        bcol[c] = jnp.broadcast_to(col, (HDIM, 128))
    same = lax.broadcasted_iota(jnp.int32, (SHARE, SHARE), 0) == lax.broadcasted_iota(
        jnp.int32, (SHARE, SHARE), 1
    )
    col = jnp.sum(jnp.where(same, fb_ref[...].reshape(1, SHARE), 0.0), axis=1, keepdims=True)
    fcol[...] = jnp.broadcast_to(col, (SHARE, 128))

    wq_copy.wait()

    def qkv(r):
        rows = gat[r].reshape(256, D)
        out = lax.dot_general(
            wqv[...], rows, (((1,), (1,)), ((), ())), preferred_element_type=jnp.float32
        )
        at = [pl.multiple_of(dev(r % 4, r // 4, p) * 128, 128) for p in range(2)]
        prow = jnp.concatenate([pos_ref[0:1, pl.ds(a, 128)] for a in at], axis=1).astype(jnp.float32)
        pcol = jnp.concatenate([pos_ref[1:2, pl.ds(a, 128)] for a in at], axis=1).astype(jnp.float32)
        row = lax.broadcasted_iota(jnp.int32, (40, 256), 0)
        power = jnp.where(row < 20, row, row - 20).astype(jnp.float32)
        inv = jnp.exp2(power * (-math.log2(10000.0) / 20.0))
        angle = jnp.where(row < 20, prow, pcol) * inv
        cos, sin = jnp.cos(angle), jnp.sin(angle)

        def turn(v):
            lo, hi = v[:40], v[40:]
            return jnp.concatenate([lo * cos - hi * sin, hi * cos + lo * sin], axis=0)

        bias = [jnp.concatenate([bcol[c], bcol[c]], axis=1) for c in range(3)]
        pad = jnp.zeros((128 - HDIM, 256), jnp.float32)
        q = turn(out[0:80] + bias[0])
        k = turn(out[80:160] + bias[1])
        v = out[160:240] + bias[2]
        qt[r] = jnp.concatenate([q, pad], axis=0).astype(jnp.bfloat16)
        kk[r] = jnp.concatenate([k, pad], axis=0).T.astype(jnp.bfloat16)
        vt[r] = v.astype(jnp.bfloat16)

    g1.wait_partner([0])
    qkv(0)
    g1.first()
    g1.wait_partner([3, 1, 4])
    for r in (3, 1, 4):
        qkv(r)
    g1.second()
    g1.wait_partner([2])
    qkv(2)
    g1.third(0)
    g1.third(1)
    wp_copy.wait()
    gw.begin()
    g1.wait_partner([5, 7, 6])
    for r in (5, 7, 6):
        qkv(r)

    def score(r, slot):
        top = None
        for kc in range(ROLES):
            s = jnp.dot(kk[kc], qt[r], preferred_element_type=jnp.float32)
            sc[slot, kc] = s
            m = jnp.max(s.reshape(32, 8, 256), axis=0)
            top = m if top is None else jnp.maximum(top, m)
        return jnp.max(top, axis=0, keepdims=True) * SCALE

    def weigh(r, slot, top):
        total, out = None, None
        for kc in range(ROLES):
            w = jnp.exp2(sc[slot, kc] * SCALE - top)
            s = jnp.sum(w.reshape(32, 8, 256), axis=0)
            o = jnp.dot(vt[kc], w.astype(jnp.bfloat16), preferred_element_type=jnp.float32)
            total = s if total is None else total + s
            out = o if out is None else out + o
        out = (out / jnp.sum(total, axis=0, keepdims=True)).astype(jnp.bfloat16)
        for p in range(2):
            osend[r, p] = out[:, p * 128 : (p + 1) * 128]

    back = []

    def give(r):
        for p in range(2):
            if r == 0 and p == 0:
                continue
            role = 4 * (r // 4) + (-r % 4) % 4
            copy = pltpu.make_async_remote_copy(
                src_ref=osend.at[r, p],
                dst_ref=att.at[role, p],
                send_sem=asend.at[r, p],
                recv_sem=arecv.at[role, p],
                device_id={"sp": dev(r % 4, r // 4, p)},
                device_id_type=MESH,
            )
            copy.start()
            back.append((copy, role, p))

    order = (6, 7, 5, 2, 4, 3, 1, 0)
    top = score(order[0], 0)
    for i, r in enumerate(order):
        if i + 1 < ROLES:
            later = score(order[i + 1], (i + 1) % 2)
        weigh(r, i % 2, top)
        top = later
        if i > 0:
            give(order[i - 1])
        if i == 3:
            gw.first()
        if i == 6:
            gw.second()
    give(order[-1])
    att[0, 0] = osend[0, 0]
    gw.third(0)
    gw.third(1)
    gw.wait_partner(range(ROLES))
    for copy, role, p in back:
        copy.wait_recv()

    got = att[...].reshape(D, 128).T
    out = jnp.dot(got, wg[...].reshape(D, D), preferred_element_type=jnp.float32)
    vit = (x_ref[...].astype(jnp.float32) + out + pb_ref[...].reshape(1, D)).astype(jnp.bfloat16)
    vitv[...] = vit
    zn = norm_rows(vit.astype(jnp.float32), g2_ref[...].reshape(1, D), b2_ref[...].reshape(1, D))
    for b in range(D // 128):
        zf[b] = zn[:, b * 128 : (b + 1) * 128]
    for j in range(4):
        for b in range(D // 128):
            blk[0, 0, j // 2, pl.ds((j % 2) * 32, 32), pl.ds(b * 128, 128)] = zf[
                b, pl.ds(j, 32, stride=4), :
            ].astype(jnp.bfloat16)

    g2.begin()
    vit_copy = pltpu.make_async_copy(vitv, vit_hbm, local.at[3])
    vit_copy.start()
    fc_copy.wait()

    def fc1(dy, h):
        total = None
        for j in (2 * h, 2 * h + 1):
            parts = []
            for ax in range(4):
                r = 4 * dy + (ax + 4 - mx) % 4
                for c in range(2):
                    parts.append(blk[r, (c + core) % 2, h, pl.ds((j % 2) * 32, 32)])
            o = lax.dot_general(
                fcv[:, j * D : (j + 1) * D],
                jnp.concatenate(parts, axis=0),
                (((1,), (1,)), ((), ())),
                preferred_element_type=jnp.float32,
            )
            total = o if total is None else total + o
        return total

    def finish(dy, total):
        v = total + jnp.concatenate([fcol[...], fcol[...]], axis=1)
        hidv[dy] = (0.5 * v * (1.0 + lax.erf(v * (2.0**-0.5)))).astype(jnp.bfloat16)
        at = pl.multiple_of(((my + dy) % 2) * 256, 256)
        copy = pltpu.make_async_copy(hidv.at[dy], hid_hbm.at[:, pl.ds(at, 256)], local.at[4 + dy])
        copy.start()
        return copy

    g2.first()
    g2.second()
    g2.wait_partner([0, 3, 1, 2])
    done0 = finish(0, fc1(0, 0) + fc1(0, 1))
    g2.third(0)
    for r in (4, 5, 7, 6):
        g2.wait(r, 1, 0)
    half = fc1(1, 0)
    g2.third(1)
    for r in (4, 5, 7, 6):
        g2.wait(r, 1, 1)
    done1 = finish(1, half + fc1(1, 1))

    for g in (g1, gw, g2):
        g.drain()
    for copy, _, _ in back:
        copy.wait_send()
    vit_copy.wait()
    done0.wait()
    done1.wait()


def per_device(
    patches, pos_ids, norm_gain, norm_bias, qkv_weight, qkv_bias, proj_weight, proj_bias, merge_gain, merge_bias,
    fc1_weight, fc1_bias,
):
    vmem = pl.BlockSpec(memory_space=pltpu.VMEM)
    hbm = pl.BlockSpec(memory_space=pl.ANY)
    bf, f32 = jnp.bfloat16, jnp.float32
    dma = pltpu.SemaphoreType.DMA
    vit, hid = pl.pallas_call(
        kernel,
        out_shape=(jax.ShapeDtypeStruct((128, D), bf), jax.ShapeDtypeStruct((SHARE, 512), bf)),
        in_specs=[vmem, vmem, vmem, vmem, hbm, vmem, hbm, vmem, vmem, vmem, hbm, vmem],
        out_specs=(hbm, hbm),
        scratch_shapes=[
            pltpu.VMEM((ROLES, 2, 2, 64, D), bf),
            pltpu.VMEM((ROLES, 2, 2, 64, D), bf),
            pltpu.VMEM((ROLES, 2, HDIM, D), bf),
            pltpu.VMEM((ROLES, 2, HDIM, 128), bf),
            pltpu.VMEM((ROLES, 2, HDIM, 128), bf),
            pltpu.VMEM((ROLES, 128, 256), bf),
            pltpu.VMEM((ROLES, 256, 128), bf),
            pltpu.VMEM((ROLES, HDIM, 256), bf),
            pltpu.VMEM((2, ROLES, 256, 256), f32),
            pltpu.VMEM((SHARE, HIDDEN), bf),
            pltpu.VMEM((3 * HDIM, D), bf),
            pltpu.VMEM((3, HDIM, 128), f32),
            pltpu.VMEM((SHARE, 128), f32),
            pltpu.VMEM((D // 128, 128, 128), f32),
            pltpu.VMEM((128, D), bf),
            pltpu.VMEM((2, SHARE, 256), bf),
            dma((3, 32)),
            dma((3, ROLES, 2, 2)),
            dma((ROLES, 2)),
            dma((ROLES, 2)),
            dma((6,)),
        ],
        compiler_params=pltpu.CompilerParams(
            collective_id=0, has_side_effects=True, vmem_limit_bytes=58 * 1024 * 1024
        ),
    )(
        patches,
        pos_ids,
        norm_gain,
        norm_bias,
        qkv_weight.transpose(1, 2, 0).reshape(3 * HDIM, D),
        qkv_bias,
        proj_weight,
        proj_bias,
        merge_gain,
        merge_bias,
        fc1_weight.T,
        fc1_bias,
    )
    return vit, hid.T


def solution(mesh):
    return jax.shard_map(
        per_device,
        mesh=mesh,
        in_specs=(
            P(("img", "sp"), None),
            P(None, "img"),
            P(),
            P(),
            P(None, None, "sp"),
            P(),
            P("sp", None),
            P(),
            P(),
            P(),
            P(None, "sp"),
            P("sp"),
        ),
        out_specs=(P(("img", "sp"), None), P("img", "sp")),
        check_vma=False,
    )
```

time: 180 us -> 82.7 us (0.46)
  waiting for transfers between devices: 109 us -> 0 us
  Pallas kernels: 0 us -> 78.4 us
  matrix products: 27.9 us -> 0 us
  other arithmetic: 14.1 us -> 0 us
  between operations: 13.8 us -> 0.64 us
  local copies, waits for them, and re-layouts: 10.3 us -> 3.44 us
  starting transfers between devices: 4.34 us -> 0 us
    all_gather x3 -> x0, waiting for transfers between devices: 108 us -> none  [the longest x1 49.5 us: per_device(): lax.all_gather(normed, 'sp', axis=0, tiled=True)]
    pallas_call x0 -> x1, Pallas kernels: none -> 78.4 us  [per_device(): pl.pallas_call(kernel, out_shape=(jax.ShapeDtypeStruct((128, D), bf), jax...]
    dot_general x10 -> x0, matrix products: 23.7 us -> none  [the longest x4 7.49 us: one_block(): jnp.einsum('bhd,khd->hbk', qpart, kshaped, preferred_element_type=jnp.flo...]
    convert_element_type x4 -> x0, other arithmetic: 6.97 us -> none  [the longest x1 3.19 us: per_device(): keys = rotate(qkv[:, 1], pos_ids, heads_local).astype(jnp.bfloat16)]
    reduce_sum x7 -> x0, other arithmetic: 5.99 us -> none  [the longest x4 3.29 us: one_block(): jnp.sum(expo, axis=-1, keepdims=True)]
    all_to_all x1 -> x0, starting transfers between devices: 4.22 us -> none  [per_device(): lax.all_to_all(attended, 'sp', split_axis=0, concat_axis=1, tiled=True)]
    unnamed x1 -> x0, matrix products: 4.17 us -> none
    all_to_all x2 -> x0, local copies, waits for them, and re-layouts: 3.61 us -> none  [per_device(): lax.all_to_all(attended, 'sp', split_axis=0, concat_axis=1, tiled=True)]
  transfers between devices with their start and end apart: 4 -> 0, of which waited for: 3 -> 0; matrix products, arithmetic and copies ran while one was open for 18% -> 0% of each run, Pallas kernels for 0% -> 0%
where the time goes in v1:
time: 82.7 us; the launch traced here: 82.5 us
  Pallas kernels  78.4 us (95%)
  local copies, waits for them, and re-layouts  3.44 us (4%)
    pallas_call x1, Pallas kernels, per_device(): pl.pallas_call(kernel, out_shape=(jax.ShapeDtypeStruct((128, D), bf), jax...  78.4 us
    unnamed x2, local copies, waits for them, and re-layouts  3.44 us

profile of v1, /device:TPU:1, one launch (start us, length us, event | category | flops | bytes accessed | tf_op | source)
XLA Modules:
  0.0 82.5 jit_solution(6840000376153251193)
XLA Ops:
  0.6 78.4 %shard_map.131 = (bf16[128,1280]{1,0:T(8,128)(2,1)}, bf16[320,512]{1,0:T(8,128)(2,1)}) custom-call(bf16[128,1280]{1,0:T(8,128)(2,1)} %x_ref.1, s32[2,2048]{1,0:T(2,128)} %pos_ref.1, f32[1280]{0:T(1024)} %g1_ref.1, f32[1280]{0:T(1024)} %b1_ref.1, bf16[240,1280]{1,0:T(8,128)(2,1)} %bitcast.6, f32[3,1280]{1,0:T(4,128)} %bq_ref.1, bf16[80,1280]{1,0:T(8,128)(2,1)} %wp_hbm.1, ...), custom_call_target="tpu_custom_call" | custom-call | tf_op jit(solution)/shard_map/pallas_call | solution.py:337
  79.1 1.7 %copy.16 = bf16[128,1280]{1,0:T(8,128)(2,1)} copy(bf16[128,1280]{1,0:T(8,128)(2,1)} %get-tuple-element.8) | data formatting | bytes 655360
  80.8 1.7 %copy.17 = bf16[512,320]{0,1:T(8,128)(2,1)} copy(bf16[512,320]{0,1:T(8,128)(2,1)} %bitcast.7) | data formatting | bytes 655360

commit v2 on v1

v2 whole, which is shorter than its diff:
```python
import math

import jax
import jax.numpy as jnp
from jax import lax
from jax.experimental import pallas as pl
from jax.experimental.pallas import tpu as pltpu
from jax.sharding import PartitionSpec as P

MESH = pl.DeviceIdType.MESH
HEADS = 16
D = 1280
HDIM = 80
PATCHES = 2048
HIDDEN = 5120
SHARE = 320
ROLES = 8
SCALE = math.log2(math.e) / math.sqrt(HDIM)


def norm_rows(v, gain, bias):
    mean = jnp.mean(v, axis=-1, keepdims=True)
    cen = v - mean
    var = jnp.mean(cen * cen, axis=-1, keepdims=True)
    return cen * lax.rsqrt(var + 1e-06) * gain + bias


def kernel(
    x_ref, pos_ref, g1_ref, b1_ref, wq_hbm, bq_ref, wp_hbm, pb_ref, g2_ref, b2_ref, fc_hbm, fb_ref,
    vit_ref, hid_ref,
    gat, blk, wg, att, osend, qt, kk, vt, sc, fcv, wqv, bcol, fcol, zf,
    ssend, srecv, precv, wsrecv, wprecv, asem, local,
):
    me = lax.axis_index("sp")
    core = me % 2
    mx = (me // 2) % 4
    my = me // 8

    def dev(dx, dy, p):
        return ((my + dy) % 2) * 8 + ((mx + dx) % 4) * 2 + (core + p) % 2

    barrier = pltpu.get_barrier_semaphore()
    for step in range(1, 16):
        pl.semaphore_signal(barrier, inc=1, device_id={"sp": (me + step) % 16}, device_id_type=MESH)

    wq_copy = pltpu.make_async_copy(wq_hbm, wqv, local.at[0])
    wp_copy = pltpu.make_async_copy(wp_hbm, wg.at[0, 0], local.at[1])
    fc_copy = pltpu.make_async_copy(fc_hbm, fcv, local.at[2])
    wq_copy.start()
    wp_copy.start()
    fc_copy.start()

    xf = x_ref[...].astype(jnp.float32)
    normed = norm_rows(xf, g1_ref[...].reshape(1, D), b1_ref[...].reshape(1, D)).astype(jnp.bfloat16)
    gat[0, 0] = normed

    pl.semaphore_wait(barrier, 15)

    class Gather:
        def __init__(self, ref, up, down, across, flow, groups, parts, srecv, precv, ssend):
            self.ref, self.up, self.down, self.across, self.flow = ref, up, down, across, flow
            self.groups, self.parts, self.srecv, self.precv, self.ssend = groups, parts, srecv, precv, ssend
            self.rows, self.here, self.sem = 0, {}, {}
            for r in range(1, ROLES):
                for g in groups[r]:
                    for i in g:
                        self.sem[r, i] = len(set(self.sem.values())) if i == g[0] else self.sem[r, g[0]]

        def copy(self, src, dst, size, at, rsem, dx, dy, p):
            return pltpu.make_async_remote_copy(
                src_ref=self.ref.at[src[0], src[1], pl.ds(at, size)],
                dst_ref=self.ref.at[dst[0], dst[1], pl.ds(at, size)],
                send_sem=self.ssend,
                recv_sem=rsem,
                device_id={"sp": dev(dx, dy, p)},
                device_id_type=MESH,
            )

        def pass_on(self, r, i, dx, dy):
            role = 4 * ((r // 4 + dy) % 2) + (r % 4 - dx) % 4
            self.copy((r, 0), (role, 0), 16, 16 * i, self.srecv.at[self.sem[role, i]], dx, dy, 0).start()
            self.rows += 16

        def share(self, r, part):
            at, size, which = self.parts[part]
            self.copy((r, 0), (r, 1), size, at, self.precv.at[r, which], 0, 0, 1).start()
            self.rows += size

        def wait(self, r, g):
            self.copy((r, 0), (r, 0), 16 * len(g), 16 * g[0], self.srecv.at[self.sem[r, g[0]]], 0, 0, 1).wait_recv()
            assert list(g) in [list(v) for v in self.groups[r]]
            if r in (1, 3) and self.across in g:
                self.pass_on(r, self.across, 0, 1)
            here = self.here.setdefault(r, set())
            for part, (at, size, _) in enumerate(self.parts):
                mine = set(range(at // 16, (at + size) // 16))
                if mine <= here | set(g) and not mine <= here:
                    self.share(r, part)
            here.update(g)

        def wait_partner(self, r, which=0):
            size = sum(v[1] for v in self.parts if v[2] == which)
            at = min(v[0] for v in self.parts if v[2] == which)
            self.copy((r, 1), (r, 1), size, at, self.precv.at[r, which], 0, 0, 1).wait_recv()

        def begin(self):
            for a, b, c in zip(self.up + self.down, self.down + self.up, self.flow):
                self.pass_on(0, a, 1, 0)
                self.pass_on(0, b, -1, 0)
                self.pass_on(0, c, 0, 1)
            for part in range(len(self.parts)):
                self.share(0, part)

        def ring(self, r, i):
            self.wait(r, [i])
            self.pass_on(r, i, 1 if r == 3 else -1, 0)

        def cross(self, g):
            self.wait(4, g)
            for i in g:
                if i != self.across:
                    self.pass_on(4, i, 1, 0)
                    self.pass_on(4, i, -1, 0)

        def rest(self):
            for r, done in ((3, self.up), (1, self.down)):
                for g in self.groups[r]:
                    if g[0] not in done:
                        self.wait(r, g)

        def far(self, i):
            self.wait(2, [i])
            self.pass_on(2, i, 0, 1)

        def last(self, g):
            for r in (5, 7, 6):
                self.wait(r, g)

        def drain(self):
            size = self.ref.shape[2]
            assert self.rows == 15 * size
            flat = self.ref.reshape(16 * size, D).at[pl.ds(0, self.rows)]
            pltpu.make_async_remote_copy(
                src_ref=flat, dst_ref=flat, send_sem=self.ssend, recv_sem=self.precv.at[0, 0],
                device_id={"sp": dev(0, 0, 1)}, device_id_type=MESH,
            ).wait_send()

    halves = [[0, 1, 2, 3], [4, 5, 6, 7]]
    groups = {
        1: [[2], [3], [6], [7], [0, 1], [4, 5]],
        2: [[i] for i in range(8)],
        3: [[0], [1], [4], [5], [2, 3], [6], [7]],
        4: halves, 5: halves, 6: halves, 7: halves,
    }
    flow = [0, 2, 1, 3, 4, 6, 5, 7]
    big = ([0, 1, 4, 5], [2, 3, 6, 7], 7, flow, groups)
    g1 = Gather(gat, *big, [(32 * j, 32, 0) for j in range(4)], srecv, precv, ssend.at[0])
    g2 = Gather(blk, *big, [(32 * j, 32, j // 2) for j in range(4)], srecv, precv, ssend.at[1])
    whole = [[0, 1, 2, 3, 4]]
    wgroups = {
        1: [[4], [3], [0, 1, 2]],
        2: [[i] for i in range(5)],
        3: [[i] for i in range(5)],
        4: [[0, 1, 2], [3, 4]], 5: whole, 6: whole, 7: whole,
    }
    gw = Gather(wg, [0, 1, 2], [4, 3], 4, [0, 1, 2, 3, 4], wgroups, [(0, 80, 0)], wsrecv, wprecv, ssend.at[2])

    g1.begin()

    lane = lax.broadcasted_iota(jnp.int32, (HDIM, D), 1)
    sub = lax.broadcasted_iota(jnp.int32, (HDIM, D), 0)
    mine = lane == sub + me * HDIM
    for c in range(3):
        col = jnp.sum(jnp.where(mine, bq_ref[c : c + 1, :], 0.0), axis=1, keepdims=True)
        bcol[c] = jnp.broadcast_to(col, (HDIM, 128))
    same = lax.broadcasted_iota(jnp.int32, (SHARE, SHARE), 0) == lax.broadcasted_iota(
        jnp.int32, (SHARE, SHARE), 1
    )
    col = jnp.sum(jnp.where(same, fb_ref[...].reshape(1, SHARE), 0.0), axis=1, keepdims=True)
    fcol[...] = jnp.broadcast_to(col, (SHARE, 128))

    wq_copy.wait()

    def qkv(r):
        rows = gat[r].reshape(256, D)
        out = lax.dot_general(
            wqv[...], rows, (((1,), (1,)), ((), ())), preferred_element_type=jnp.float32
        )
        at = [pl.multiple_of(dev(r % 4, r // 4, p) * 128, 128) for p in range(2)]
        prow = jnp.concatenate([pos_ref[0:1, pl.ds(a, 128)] for a in at], axis=1).astype(jnp.float32)
        pcol = jnp.concatenate([pos_ref[1:2, pl.ds(a, 128)] for a in at], axis=1).astype(jnp.float32)
        row = lax.broadcasted_iota(jnp.int32, (40, 256), 0)
        power = jnp.where(row < 20, row, row - 20).astype(jnp.float32)
        inv = jnp.exp2(power * (-math.log2(10000.0) / 20.0))
        angle = jnp.where(row < 20, prow, pcol) * inv
        cos, sin = jnp.cos(angle), jnp.sin(angle)

        def turn(v):
            lo, hi = v[:40], v[40:]
            return jnp.concatenate([lo * cos - hi * sin, hi * cos + lo * sin], axis=0)

        bias = [jnp.concatenate([bcol[c], bcol[c]], axis=1) for c in range(3)]
        pad = jnp.zeros((128 - HDIM, 256), jnp.float32)
        q = turn(out[0:80] + bias[0])
        k = turn(out[80:160] + bias[1])
        v = out[160:240] + bias[2]
        qt[r] = jnp.concatenate([q, pad], axis=0).astype(jnp.bfloat16)
        kk[r] = jnp.concatenate([k, pad], axis=0).T.astype(jnp.bfloat16)
        vt[r] = v.astype(jnp.bfloat16)

    with jax.named_scope("a_own"):
        g1.wait_partner(0)
        qkv(0)
    with jax.named_scope("a_ring"):
        for i, j in zip(g1.up, g1.down):
            g1.ring(3, i)
            g1.ring(1, j)
    with jax.named_scope("a_cross"):
        g1.cross(halves[0])
    with jax.named_scope("a_rest"):
        g1.rest()
        g1.cross(halves[1])
    with jax.named_scope("a_far"):
        for i in flow:
            g1.far(i)
    with jax.named_scope("a_wbegin"):
        wp_copy.wait()
        gw.begin()
    with jax.named_scope("a_qkv"):
        for r in (3, 1, 4, 2):
            g1.wait_partner(r)
            qkv(r)
    with jax.named_scope("a_last0"):
        g1.last(halves[0])
    with jax.named_scope("a_last1"):
        g1.last(halves[1])
    with jax.named_scope("w_ring0"):
        gw.ring(3, 0)
        gw.ring(1, 4)
    with jax.named_scope("a_qkv2"):
        g1.wait_partner(5)
        qkv(5)
        g1.wait_partner(7)
        qkv(7)
    with jax.named_scope("w_ring1"):
        gw.ring(3, 1)
        gw.ring(1, 3)
    with jax.named_scope("a_qkv3"):
        g1.wait_partner(6)
        qkv(6)

    def score(r, slot):
        top = None
        for kc in range(ROLES):
            s = jnp.dot(kk[kc], qt[r], preferred_element_type=jnp.float32)
            sc[slot, kc] = s
            m = jnp.max(s.reshape(32, 8, 256), axis=0)
            top = m if top is None else jnp.maximum(top, m)
        return jnp.max(top, axis=0, keepdims=True) * SCALE

    def weigh(r, slot, top):
        total, out = None, None
        for kc in range(ROLES):
            w = jnp.exp2(sc[slot, kc] * SCALE - top)
            s = jnp.sum(w.reshape(32, 8, 256), axis=0)
            o = jnp.dot(vt[kc], w.astype(jnp.bfloat16), preferred_element_type=jnp.float32)
            total = s if total is None else total + s
            out = o if out is None else out + o
        out = (out / jnp.sum(total, axis=0, keepdims=True)).astype(jnp.bfloat16)
        for p in range(2):
            osend[2 * r + p] = out[:, p * 128 : (p + 1) * 128]

    def give(r):
        for p in range(2):
            if r == 0 and p == 0:
                continue
            role = 4 * (r // 4) + (-r % 4) % 4
            pltpu.make_async_remote_copy(
                src_ref=osend.at[2 * r + p],
                dst_ref=att.at[2 * role + p],
                send_sem=asem.at[0],
                recv_sem=asem.at[1],
                device_id={"sp": dev(r % 4, r // 4, p)},
                device_id_type=MESH,
            ).start()

    order = (6, 7, 5, 2, 4, 3, 1, 0)
    top = score(order[0], 0)
    for i, r in enumerate(order):
        if i + 1 < ROLES:
            later = score(order[i + 1], (i + 1) % 2)
        weigh(r, i % 2, top)
        top = later
        if i > 0:
            give(order[i - 1])
        with jax.named_scope(f"w_tile{i}"):
            if i == 0:
                gw.ring(3, 2)
            if i == 1:
                gw.cross([0, 1, 2])
            if i == 2:
                gw.cross([3, 4])
                gw.rest()
            if i == 3:
                gw.far(0)
                gw.far(4)
            if i == 4:
                gw.far(1)
                gw.far(3)
            if i == 5:
                gw.far(2)
    with jax.named_scope("t_give"):
        give(order[-1])
        att[0] = osend[0]
    with jax.named_scope("w_last"):
        gw.last(whole[0])
    with jax.named_scope("w_partner"):
        for r in range(ROLES):
            gw.wait_partner(r)
    with jax.named_scope("t_back"):
        pltpu.make_async_remote_copy(
            src_ref=osend.at[pl.ds(1, 15)], dst_ref=att.at[pl.ds(1, 15)], send_sem=asem.at[0], recv_sem=asem.at[1],
            device_id={"sp": dev(0, 0, 1)}, device_id_type=MESH,
        ).wait_recv()

    got = att[...].reshape(D, 128).T
    out = jnp.dot(got, wg[...].reshape(D, D), preferred_element_type=jnp.float32)
    vit = (x_ref[...].astype(jnp.float32) + out + pb_ref[...].reshape(1, D)).astype(jnp.bfloat16)
    vit_ref[...] = vit
    zn = norm_rows(vit.astype(jnp.float32), g2_ref[...].reshape(1, D), b2_ref[...].reshape(1, D))
    for b in range(D // 128):
        zf[b] = zn[:, b * 128 : (b + 1) * 128]
    for j in range(4):
        for b in range(D // 128):
            blk[0, 0, pl.ds(j * 32, 32), pl.ds(b * 128, 128)] = zf[
                b, pl.ds(j, 32, stride=4), :
            ].astype(jnp.bfloat16)

    g2.begin()
    fc_copy.wait()

    def fc1(dy, j):
        parts = []
        for ax in range(4):
            r = 4 * dy + (ax + 4 - mx) % 4
            for c in range(2):
                parts.append(blk[r, (c + core) % 2, pl.ds(j * 32, 32)])
        return lax.dot_general(
            fcv[:, j * D : (j + 1) * D],
            jnp.concatenate(parts, axis=0),
            (((1,), (1,)), ((), ())),
            preferred_element_type=jnp.float32,
        )

    def finish(dy, total):
        v = total + jnp.concatenate([fcol[...], fcol[...]], axis=1)
        at = pl.multiple_of(((my + dy) % 2) * 256, 256)
        hid_ref[:, pl.ds(at, 256)] = (0.5 * v * (1.0 + lax.erf(v * (2.0**-0.5)))).astype(jnp.bfloat16)

    with jax.named_scope("b_ring"):
        for i, j in zip(g2.up, g2.down):
            g2.ring(3, i)
            g2.ring(1, j)
    with jax.named_scope("b_cross"):
        g2.cross(halves[0])
    with jax.named_scope("b_rest"):
        g2.rest()
        g2.cross(halves[1])
    with jax.named_scope("b_far"):
        for i in flow:
            g2.far(i)
    with jax.named_scope("b_far_p"):
        for r in (0, 3, 1, 2):
            g2.wait_partner(r, 0)
            g2.wait_partner(r, 1)
    with jax.named_scope("b_fc1"):
        finish(0, fc1(0, 0) + fc1(0, 1) + fc1(0, 2) + fc1(0, 3))
    with jax.named_scope("b_last0"):
        g2.last(halves[0])
    with jax.named_scope("b_last0_p"):
        for r in (4, 5, 7, 6):
            g2.wait_partner(r, 0)
    with jax.named_scope("b_fc1_0"):
        half = fc1(1, 0) + fc1(1, 1)
    with jax.named_scope("b_last1"):
        g2.last(halves[1])
    with jax.named_scope("b_last1_p"):
        for r in (4, 5, 7, 6):
            g2.wait_partner(r, 1)
    with jax.named_scope("b_fc1_1"):
        finish(1, half + fc1(1, 2) + fc1(1, 3))

    with jax.named_scope("drain"):
        for g in (g1, gw, g2):
            g.drain()
        pltpu.make_async_remote_copy(
            src_ref=osend.at[pl.ds(1, 15)], dst_ref=att.at[pl.ds(1, 15)], send_sem=asem.at[0], recv_sem=asem.at[1],
            device_id={"sp": dev(0, 0, 1)}, device_id_type=MESH,
        ).wait_send()


def per_device(
    patches, pos_ids, norm_gain, norm_bias, qkv_weight, qkv_bias, proj_weight, proj_bias, merge_gain, merge_bias,
    fc1_weight, fc1_bias,
):
    vmem = pl.BlockSpec(memory_space=pltpu.VMEM)
    hbm = pl.BlockSpec(memory_space=pl.ANY)
    bf, f32 = jnp.bfloat16, jnp.float32
    dma = pltpu.SemaphoreType.DMA
    vit, hid = pl.pallas_call(
        kernel,
        out_shape=(pltpu.VMEM((128, D), bf), pltpu.VMEM((SHARE, 512), bf)),
        in_specs=[vmem, vmem, vmem, vmem, hbm, vmem, hbm, vmem, vmem, vmem, hbm, vmem],
        out_specs=(vmem, vmem),
        scratch_shapes=[
            pltpu.VMEM((ROLES, 2, 128, D), bf),
            pltpu.VMEM((ROLES, 2, 128, D), bf),
            pltpu.VMEM((ROLES, 2, HDIM, D), bf),
            pltpu.VMEM((2 * ROLES, HDIM, 128), bf),
            pltpu.VMEM((2 * ROLES, HDIM, 128), bf),
            pltpu.VMEM((ROLES, 128, 256), bf),
            pltpu.VMEM((ROLES, 256, 128), bf),
            pltpu.VMEM((ROLES, HDIM, 256), bf),
            pltpu.VMEM((2, ROLES, 256, 256), f32),
            pltpu.VMEM((SHARE, HIDDEN), bf),
            pltpu.VMEM((3 * HDIM, D), bf),
            pltpu.VMEM((3, HDIM, 128), f32),
            pltpu.VMEM((SHARE, 128), f32),
            pltpu.VMEM((D // 128, 128, 128), f32),
            dma((3,)),
            dma((29,)),
            dma((ROLES, 2)),
            dma((18,)),
            dma((ROLES, 1)),
            dma((2,)),
            dma((3,)),
        ],
        compiler_params=pltpu.CompilerParams(
            collective_id=0, has_side_effects=True, vmem_limit_bytes=58 * 1024 * 1024
        ),
    )(
        patches,
        pos_ids,
        norm_gain,
        norm_bias,
        qkv_weight.transpose(1, 2, 0).reshape(3 * HDIM, D),
        qkv_bias,
        proj_weight,
        proj_bias,
        merge_gain,
        merge_bias,
        fc1_weight.T,
        fc1_bias,
    )
    return vit, hid.T


def solution(mesh):
    return jax.shard_map(
        per_device,
        mesh=mesh,
        in_specs=(
            P(("img", "sp"), None),
            P(None, "img"),
            P(),
            P(),
            P(None, None, "sp"),
            P(),
            P("sp", None),
            P(),
            P(),
            P(),
            P(None, "sp"),
            P("sp"),
        ),
        out_specs=(P(("img", "sp"), None), P("img", "sp")),
        check_vma=False,
    )
```

time: 82.7 us -> 72.5 us (0.88)
  Pallas kernels: 78.4 us -> 70.3 us
  local copies, waits for them, and re-layouts: 3.44 us -> 1.45 us
    pallas_call x1, Pallas kernels: 78.4 us -> 70.3 us  [per_device(): pl.pallas_call(kernel, out_shape=(pltpu.VMEM((128, D), bf), pltpu.VMEM((S...]
    unnamed x2, local copies, waits for them, and re-layouts: 3.44 us -> 1.45 us
where the time goes in v2:
time: 72.5 us; the launch traced here: 72.4 us
  Pallas kernels  70.3 us (97%)
  local copies, waits for them, and re-layouts  1.45 us (2%)
    pallas_call x1, Pallas kernels, per_device(): pl.pallas_call(kernel, out_shape=(pltpu.VMEM((128, D), bf), pltpu.VMEM((S...  70.3 us
    unnamed x2, local copies, waits for them, and re-layouts  1.45 us

profile of v2, /device:TPU:1, one launch (start us, length us, event | category | flops | bytes accessed | tf_op | source)
XLA Modules:
  0.0 72.4 jit_solution(6104827476164922533)
XLA Ops:
  0.6 70.3 %shard_map.131 = (bf16[128,1280]{1,0:T(8,128)(2,1)S(1)}, bf16[320,512]{1,0:T(8,128)(2,1)S(1)}) custom-call(bf16[128,1280]{1,0:T(8,128)(2,1)} %x_ref.1, s32[2,2048]{1,0:T(2,128)} %pos_ref.1, f32[1280]{0:T(1024)} %g1_ref.1, f32[1280]{0:T(1024)} %b1_ref.1, bf16[240,1280]{1,0:T(8,128)(2,1)} %bitcast.7, f32[3,1280]{1,0:T(4,128)} %bq_ref.1, ...), custom_call_target="tpu_custom_call" | custom-call | tf_op jit(solution)/shard_map/pallas_call | solution.py:410
  71.0 0.7 %copy.16 = bf16[128,1280]{1,0:T(8,128)(2,1)} copy(bf16[128,1280]{1,0:T(8,128)(2,1)S(1)} %get-tuple-element.6) | data formatting | bytes 655360
  71.7 0.7 copy.17

commit v3 on v2

--- a/solution.py
+++ b/solution.py
@@ -26,12 +26,13 @@
 
 
 def kernel(
-    x_ref, pos_ref, g1_ref, b1_ref, wq_hbm, bq_ref, wp_hbm, pb_ref, g2_ref, b2_ref, fc_hbm, fb_ref,
-    vit_ref, hid_ref,
+    x_hbm, pos_hbm, g1_hbm, b1_hbm, wq_hbm, bq_hbm, wp_hbm, pb_hbm, g2_hbm, b2_hbm, fc_hbm, fb_hbm,
+    vit_ref, hid_ref, x_ref, pos_ref, g1_ref, b1_ref, bq_ref, pb_ref, g2_ref, b2_ref, fb_ref,
     gat, blk, wg, att, osend, qt, kk, vt, sc, fcv, wqv, bcol, fcol, zf,
     ssend, srecv, precv, wsrecv, wprecv, asem, local,
 ):
     me = lax.axis_index("sp")
+    img, images = lax.axis_index("img"), lax.axis_size("img")
     core = me % 2
     mx = (me // 2) % 4
     my = me // 8
@@ -40,21 +41,29 @@
         return ((my + dy) % 2) * 8 + ((mx + dx) % 4) * 2 + (core + p) % 2
 
     barrier = pltpu.get_barrier_semaphore()
-    for step in range(1, 16):
-        pl.semaphore_signal(barrier, inc=1, device_id={"sp": (me + step) % 16}, device_id_type=MESH)
-
-    wq_copy = pltpu.make_async_copy(wq_hbm, wqv, local.at[0])
-    wp_copy = pltpu.make_async_copy(wp_hbm, wg.at[0, 0], local.at[1])
-    fc_copy = pltpu.make_async_copy(fc_hbm, fcv, local.at[2])
-    wq_copy.start()
-    wp_copy.start()
-    fc_copy.start()
-
+    for near in (dev(1, 0, 0), dev(-1, 0, 0), dev(0, 1, 0), dev(0, 0, 1)):
+        pl.semaphore_signal(barrier, inc=1, device_id={"img": img, "sp": near}, device_id_type=MESH)
+    pl.semaphore_signal(barrier, inc=1, device_id={"img": (img + images // 2) % images, "sp": dev(0, 1, 0)}, device_id_type=MESH)
+
+    loads = [
+        (x_hbm, x_ref), (g1_hbm, g1_ref), (b1_hbm, b1_ref), (wp_hbm, wg.at[0, 0]), (bq_hbm, bq_ref), (fb_hbm, fb_ref),
+        (wq_hbm, wqv), (pos_hbm, pos_ref), (pb_hbm, pb_ref), (g2_hbm, g2_ref), (b2_hbm, b2_ref), (fc_hbm, fcv),
+    ]
+    loads = [pltpu.make_async_copy(src, dst, local.at[i]) for i, (src, dst) in enumerate(loads)]
+    for load in loads:
+        load.start()
+    for load in loads[:3]:
+        load.wait()
+
+    ln_scope = jax.named_scope("s_ln")
+    ln_scope.__enter__()
     xf = x_ref[...].astype(jnp.float32)
     normed = norm_rows(xf, g1_ref[...].reshape(1, D), b1_ref[...].reshape(1, D)).astype(jnp.bfloat16)
     gat[0, 0] = normed
-
-    pl.semaphore_wait(barrier, 15)
+    ln_scope.__exit__(None, None, None)
+
+    with jax.named_scope("s_bar"):
+        pl.semaphore_wait(barrier, 5)
 
     class Gather:
         def __init__(self, ref, up, down, across, flow, groups, parts, srecv, precv, ssend):
@@ -66,19 +75,19 @@
                     for i in g:
                         self.sem[r, i] = len(set(self.sem.values())) if i == g[0] else self.sem[r, g[0]]
 
-        def copy(self, src, dst, size, at, rsem, dx, dy, p):
+        def copy(self, src, dst, size, at, rsem, dx, dy, p, other=False):
             return pltpu.make_async_remote_copy(
                 src_ref=self.ref.at[src[0], src[1], pl.ds(at, size)],
                 dst_ref=self.ref.at[dst[0], dst[1], pl.ds(at, size)],
                 send_sem=self.ssend,
                 recv_sem=rsem,
-                device_id={"sp": dev(dx, dy, p)},
+                device_id={"img": (img + images // 2) % images if other else img, "sp": dev(dx, dy, p)},
                 device_id_type=MESH,
             )
 
-        def pass_on(self, r, i, dx, dy):
+        def pass_on(self, r, i, dx, dy, other=False):
             role = 4 * ((r // 4 + dy) % 2) + (r % 4 - dx) % 4
-            self.copy((r, 0), (role, 0), 16, 16 * i, self.srecv.at[self.sem[role, i]], dx, dy, 0).start()
+            self.copy((r, 0), (role, 0), 16, 16 * i, self.srecv.at[self.sem[role, i]], dx, dy, 0, other).start()
             self.rows += 16
 
         def share(self, r, part):
@@ -103,13 +112,29 @@
             at = min(v[0] for v in self.parts if v[2] == which)
             self.copy((r, 1), (r, 1), size, at, self.precv.at[r, which], 0, 0, 1).wait_recv()
 
-        def begin(self):
-            for a, b, c in zip(self.up + self.down, self.down + self.up, self.flow):
+        def own(self, lo, hi):
+            for a, b in list(zip(self.up + self.down, self.down + self.up))[lo:hi]:
                 self.pass_on(0, a, 1, 0)
                 self.pass_on(0, b, -1, 0)
-                self.pass_on(0, c, 0, 1)
+
+        def share_own(self):
             for part in range(len(self.parts)):
                 self.share(0, part)
+
+        def begin(self):
+            self.own(0, 2)
+            for n, c in enumerate(self.flow):
+                self.pass_on(0, c, 0, 1)
+                if n in (1, 3, 5, 7):
+                    self.own(2 + n // 2, 3 + n // 2)
+            self.share_own()
+
+        def ring_all(self):
+            for n, (i, j) in enumerate(zip(self.up, self.down)):
+                self.ring(3, i)
+                self.ring(1, j)
+                if n in (1, 3):
+                    self.own(6 + n // 2, 7 + n // 2)
 
         def ring(self, r, i):
             self.wait(r, [i])
@@ -146,27 +171,55 @@
             ).wait_send()
 
     halves = [[0, 1, 2, 3], [4, 5, 6, 7]]
+    pairs = [[0, 1], [2, 3], [4, 5], [6, 7]]
     groups = {
         1: [[2], [3], [6], [7], [0, 1], [4, 5]],
         2: [[i] for i in range(8)],
         3: [[0], [1], [4], [5], [2, 3], [6], [7]],
-        4: halves, 5: halves, 6: halves, 7: halves,
+        4: halves, 5: pairs, 6: pairs, 7: pairs,
     }
     flow = [0, 2, 1, 3, 4, 6, 5, 7]
     big = ([0, 1, 4, 5], [2, 3, 6, 7], 7, flow, groups)
     g1 = Gather(gat, *big, [(32 * j, 32, 0) for j in range(4)], srecv, precv, ssend.at[0])
-    g2 = Gather(blk, *big, [(32 * j, 32, j // 2) for j in range(4)], srecv, precv, ssend.at[1])
+    g2 = Gather(blk, *big, [(32 * j, 32, j) for j in range(4)], srecv, precv, ssend.at[1])
     whole = [[0, 1, 2, 3, 4]]
+    two = [[0, 1, 2], [3, 4]]
     wgroups = {
-        1: [[4], [3], [0, 1, 2]],
+        1: [[4], [3], [2], [0, 1]],
         2: [[i] for i in range(5)],
-        3: [[i] for i in range(5)],
-        4: [[0, 1, 2], [3, 4]], 5: whole, 6: whole, 7: whole,
+        3: [[0], [1], [2], [3, 4]],
+        4: whole, 5: two, 6: two, 7: two,
     }
-    gw = Gather(wg, [0, 1, 2], [4, 3], 4, [0, 1, 2, 3, 4], wgroups, [(0, 80, 0)], wsrecv, wprecv, ssend.at[2])
+    gw = Gather(wg, [0, 1, 2], [4, 3], None, None, wgroups, [(0, 48, 0), (48, 32, 0)], wsrecv, wprecv, ssend.at[2])
+
+    def w_near(r, g):
+        gw.wait(r, g)
+        for i in g:
+            if i in (gw.up if r == 3 else gw.down):
+                gw.pass_on(r, i, 1 if r == 3 else -1, 0)
+        for i in g:
+            if i in ((0, 1, 2) if r == 3 else (4, 3, 2)):
+                gw.pass_on(r, i, 0, 1, r == 3)
+
+    def w_cross():
+        gw.wait(4, whole[0])
+        for i in (0, 1):
+            gw.pass_on(4, i, -1, 0)
+        for i in (4, 3):
+            gw.pass_on(4, i, 1, 0)
+
+    def w_far(i):
+        gw.wait(2, [i])
+        gw.pass_on(2, i, 0, 1, i != 0)
 
     g1.begin()
-
+    loads[3].wait()
+    for i in range(5):
+        gw.pass_on(0, i, 0, 1, True)
+    gw.share_own()
+
+    for load in loads[4:6]:
+        load.wait()
     lane = lax.broadcasted_iota(jnp.int32, (HDIM, D), 1)
     sub = lax.broadcasted_iota(jnp.int32, (HDIM, D), 0)
     mine = lane == sub + me * HDIM
@@ -179,17 +232,19 @@
     col = jnp.sum(jnp.where(same, fb_ref[...].reshape(1, SHARE), 0.0), axis=1, keepdims=True)
     fcol[...] = jnp.broadcast_to(col, (SHARE, 128))
 
-    wq_copy.wait()
-
-    def qkv(r):
-        rows = gat[r].reshape(256, D)
+    for load in loads[6:8]:
+        load.wait()
+
+    def qkv(r, ps=(0, 1)):
+        n = 128 * len(ps)
+        rows = gat[r, ps[0] : ps[-1] + 1].reshape(n, D)
         out = lax.dot_general(
             wqv[...], rows, (((1,), (1,)), ((), ())), preferred_element_type=jnp.float32
         )
-        at = [pl.multiple_of(dev(r % 4, r // 4, p) * 128, 128) for p in range(2)]
+        at = [pl.multiple_of(dev(r % 4, r // 4, p) * 128, 128) for p in ps]
         prow = jnp.concatenate([pos_ref[0:1, pl.ds(a, 128)] for a in at], axis=1).astype(jnp.float32)
         pcol = jnp.concatenate([pos_ref[1:2, pl.ds(a, 128)] for a in at], axis=1).astype(jnp.float32)
-        row = lax.broadcasted_iota(jnp.int32, (40, 256), 0)
+        row = lax.broadcasted_iota(jnp.int32, (40, n), 0)
         power = jnp.where(row < 20, row, row - 20).astype(jnp.float32)
         inv = jnp.exp2(power * (-math.log2(10000.0) / 20.0))
         angle = jnp.where(row < 20, prow, pcol) * inv
@@ -199,55 +254,60 @@
             lo, hi = v[:40], v[40:]
             return jnp.concatenate([lo * cos - hi * sin, hi * cos + lo * sin], axis=0)
 
-        bias = [jnp.concatenate([bcol[c], bcol[c]], axis=1) for c in range(3)]
-        pad = jnp.zeros((128 - HDIM, 256), jnp.float32)
+        bias = [jnp.concatenate([bcol[c]] * len(ps), axis=1) for c in range(3)]
+        pad = jnp.zeros((128 - HDIM, n), jnp.float32)
         q = turn(out[0:80] + bias[0])
         k = turn(out[80:160] + bias[1])
         v = out[160:240] + bias[2]
-        qt[r] = jnp.concatenate([q, pad], axis=0).astype(jnp.bfloat16)
-        kk[r] = jnp.concatenate([k, pad], axis=0).T.astype(jnp.bfloat16)
-        vt[r] = v.astype(jnp.bfloat16)
+        where = pl.ds(ps[0] * 128, n)
+        qt[r, :, where] = jnp.concatenate([q, pad], axis=0).astype(jnp.bfloat16)
+        kk[r, where] = jnp.concatenate([k, pad], axis=0).T.astype(jnp.bfloat16)
+        vt[r, :, where] = v.astype(jnp.bfloat16)
 
     with jax.named_scope("a_own"):
         g1.wait_partner(0)
         qkv(0)
     with jax.named_scope("a_ring"):
-        for i, j in zip(g1.up, g1.down):
-            g1.ring(3, i)
-            g1.ring(1, j)
+        g1.ring_all()
     with jax.named_scope("a_cross"):
         g1.cross(halves[0])
+    with jax.named_scope("a_far0"):
+        for i in flow[:4]:
+            g1.far(i)
+    with jax.named_scope("a_cross1"):
+        g1.cross(halves[1])
+    with jax.named_scope("a_far1"):
+        for i in flow[4:]:
+            g1.far(i)
+    with jax.named_scope("a_wbegin"):
+        gw.own(0, 5)
     with jax.named_scope("a_rest"):
         g1.rest()
-        g1.cross(halves[1])
-    with jax.named_scope("a_far"):
-        for i in flow:
-            g1.far(i)
-    with jax.named_scope("a_wbegin"):
-        wp_copy.wait()
-        gw.begin()
     with jax.named_scope("a_qkv"):
-        for r in (3, 1, 4, 2):
+        for n, r in enumerate((3, 1, 4, 2)):
             g1.wait_partner(r)
             qkv(r)
-    with jax.named_scope("a_last0"):
-        g1.last(halves[0])
-    with jax.named_scope("a_last1"):
-        g1.last(halves[1])
+            if n > 0:
+                g1.last(pairs[n - 1])
+    with jax.named_scope("a_last"):
+        g1.last(pairs[3])
     with jax.named_scope("w_ring0"):
-        gw.ring(3, 0)
-        gw.ring(1, 4)
+        w_near(3, [0])
+        w_near(1, [4])
+        w_cross()
     with jax.named_scope("a_qkv2"):
-        g1.wait_partner(5)
-        qkv(5)
-        g1.wait_partner(7)
-        qkv(7)
+        for r in (5, 7, 6):
+            qkv(r, (0,))
     with jax.named_scope("w_ring1"):
-        gw.ring(3, 1)
-        gw.ring(1, 3)
+        w_near(3, [1])
+        w_near(1, [3])
     with jax.named_scope("a_qkv3"):
-        g1.wait_partner(6)
-        qkv(6)
+        for r in (5, 7, 6):
+            g1.wait_partner(r)
+            qkv(r, (1,))
+    with jax.named_scope("w_ring2"):
+        w_near(3, [2])
+        w_near(1, [2])
 
     def score(r, slot):
         top = None
@@ -294,26 +354,23 @@
         if i > 0:
             give(order[i - 1])
         with jax.named_scope(f"w_tile{i}"):
-            if i == 0:
-                gw.ring(3, 2)
             if i == 1:
-                gw.cross([0, 1, 2])
-            if i == 2:
-                gw.cross([3, 4])
-                gw.rest()
+                w_near(3, [3, 4])
+                w_near(1, [0, 1])
             if i == 3:
-                gw.far(0)
-                gw.far(4)
+                w_far(0)
+                w_far(4)
             if i == 4:
-                gw.far(1)
-                gw.far(3)
+                w_far(1)
+                w_far(3)
             if i == 5:
-                gw.far(2)
+                w_far(2)
     with jax.named_scope("t_give"):
         give(order[-1])
         att[0] = osend[0]
     with jax.named_scope("w_last"):
-        gw.last(whole[0])
+        gw.last(two[0])
+        gw.last(two[1])
     with jax.named_scope("w_partner"):
         for r in range(ROLES):
             gw.wait_partner(r)
@@ -323,6 +380,8 @@
             device_id={"sp": dev(0, 0, 1)}, device_id_type=MESH,
         ).wait_recv()
 
+    for load in loads[8:11]:
+        load.wait()
     got = att[...].reshape(D, 128).T
     out = jnp.dot(got, wg[...].reshape(D, D), preferred_element_type=jnp.float32)
     vit = (x_ref[...].astype(jnp.float32) + out + pb_ref[...].reshape(1, D)).astype(jnp.bfloat16)
@@ -337,7 +396,7 @@
             ].astype(jnp.bfloat16)
 
     g2.begin()
-    fc_copy.wait()
+    loads[11].wait()
 
     def fc1(dy, j):
         parts = []
@@ -358,37 +417,52 @@
         hid_ref[:, pl.ds(at, 256)] = (0.5 * v * (1.0 + lax.erf(v * (2.0**-0.5)))).astype(jnp.bfloat16)
 
     with jax.named_scope("b_ring"):
-        for i, j in zip(g2.up, g2.down):
-            g2.ring(3, i)
-            g2.ring(1, j)
+        g2.ring_all()
     with jax.named_scope("b_cross"):
         g2.cross(halves[0])
+    with jax.named_scope("b_far0"):
+        for i in flow[:4]:
+            g2.far(i)
+    with jax.named_scope("b_cross1"):
+        g2.cross(halves[1])
+    with jax.named_scope("b_far1"):
+        for i in flow[4:]:
+            g2.far(i)
     with jax.named_scope("b_rest"):
         g2.rest()
-        g2.cross(halves[1])
-    with jax.named_scope("b_far"):
-        for i in flow:
-            g2.far(i)
+    def partner(j):
+        with jax.named_scope(f"b_partner{j}"):
+            for r in (5, 7, 6):
+                g2.wait_partner(r, j)
+
+    with jax.named_scope("b_last0"):
+        g2.last(pairs[0])
     with jax.named_scope("b_far_p"):
-        for r in (0, 3, 1, 2):
-            g2.wait_partner(r, 0)
-            g2.wait_partner(r, 1)
-    with jax.named_scope("b_fc1"):
-        finish(0, fc1(0, 0) + fc1(0, 1) + fc1(0, 2) + fc1(0, 3))
-    with jax.named_scope("b_last0"):
-        g2.last(halves[0])
-    with jax.named_scope("b_last0_p"):
-        for r in (4, 5, 7, 6):
-            g2.wait_partner(r, 0)
-    with jax.named_scope("b_fc1_0"):
-        half = fc1(1, 0) + fc1(1, 1)
+        for r in (0, 3, 1, 2, 4):
+            for j in range(4):
+                g2.wait_partner(r, j)
+    with jax.named_scope("b_fc1_a"):
+        total = fc1(0, 0) + fc1(0, 1)
     with jax.named_scope("b_last1"):
-        g2.last(halves[1])
-    with jax.named_scope("b_last1_p"):
-        for r in (4, 5, 7, 6):
-            g2.wait_partner(r, 1)
-    with jax.named_scope("b_fc1_1"):
-        finish(1, half + fc1(1, 2) + fc1(1, 3))
+        g2.last(pairs[1])
+    with jax.named_scope("b_fc1_b"):
+        finish(0, total + fc1(0, 2) + fc1(0, 3))
+    partner(0)
+    with jax.named_scope("b_fc1_c"):
+        total = fc1(1, 0)
+    with jax.named_scope("b_last2"):
+        g2.last(pairs[2])
+    with jax.named_scope("b_last3"):
+        g2.last(pairs[3])
+    partner(1)
+    with jax.named_scope("b_fc1_d"):
+        total = total + fc1(1, 1)
+    partner(2)
+    with jax.named_scope("b_fc1_e"):
+        total = total + fc1(1, 2)
+    partner(3)
+    with jax.named_scope("b_fc1_f"):
+        finish(1, total + fc1(1, 3))
 
     with jax.named_scope("drain"):
         for g in (g1, gw, g2):
@@ -410,9 +484,18 @@
     vit, hid = pl.pallas_call(
         kernel,
         out_shape=(pltpu.VMEM((128, D), bf), pltpu.VMEM((SHARE, 512), bf)),
-        in_specs=[vmem, vmem, vmem, vmem, hbm, vmem, hbm, vmem, vmem, vmem, hbm, vmem],
+        in_specs=[hbm] * 12,
         out_specs=(vmem, vmem),
         scratch_shapes=[
+            pltpu.VMEM((128, D), bf),
+            pltpu.VMEM((2, PATCHES), jnp.int32),
+            pltpu.VMEM((D,), f32),
+            pltpu.VMEM((D,), f32),
+            pltpu.VMEM((3, D), f32),
+            pltpu.VMEM((D,), f32),
+            pltpu.VMEM((D,), f32),
+            pltpu.VMEM((D,), f32),
+            pltpu.VMEM((SHARE,), f32),
             pltpu.VMEM((ROLES, 2, 128, D), bf),
             pltpu.VMEM((ROLES, 2, 128, D), bf),
             pltpu.VMEM((ROLES, 2, HDIM, D), bf),
@@ -428,12 +511,12 @@
             pltpu.VMEM((SHARE, 128), f32),
             pltpu.VMEM((D // 128, 128, 128), f32),
             dma((3,)),
-            dma((29,)),
-            dma((ROLES, 2)),
-            dma((18,)),
+            dma((35,)),
+            dma((ROLES, 4)),
+            dma((20,)),
             dma((ROLES, 1)),
             dma((2,)),
-            dma((3,)),
+            dma((12,)),
         ],
         compiler_params=pltpu.CompilerParams(
             collective_id=0, has_side_effects=True, vmem_limit_bytes=58 * 1024 * 1024

time: 72.5 us -> 66.4 us (0.916)
  Pallas kernels: 70.3 us -> 64.2 us
    pallas_call x1, Pallas kernels: 70.3 us -> 64.2 us  [per_device(): pl.pallas_call(kernel, out_shape=(pltpu.VMEM((128, D), bf), pltpu.VMEM((S...]
where the time goes in v3:
time: 66.4 us; the launch traced here: 66.2 us
  Pallas kernels  64.2 us (97%)
  local copies, waits for them, and re-layouts  1.45 us (2%)
    pallas_call x1, Pallas kernels, per_device(): pl.pallas_call(kernel, out_shape=(pltpu.VMEM((128, D), bf), pltpu.VMEM((S...  64.2 us
    unnamed x2, local copies, waits for them, and re-layouts  1.45 us

profile of v3, /device:TPU:1, one launch (start us, length us, event | category | flops | bytes accessed | tf_op | source)
XLA Modules:
  0.0 66.2 jit_solution(17575374315871678329)
XLA Ops:
  0.6 64.2 %shard_map.131 = (bf16[128,1280]{1,0:T(8,128)(2,1)S(1)}, bf16[320,512]{1,0:T(8,128)(2,1)S(1)}) custom-call(bf16[128,1280]{1,0:T(8,128)(2,1)} %x_hbm.1, s32[2,2048]{1,0:T(2,128)} %pos_hbm.1, f32[1280]{0:T(1024)} %g1_hbm.1, f32[1280]{0:T(1024)} %b1_hbm.1, bf16[240,1280]{1,0:T(8,128)(2,1)} %bitcast.7, f32[3,1280]{1,0:T(4,128)} %bq_hbm.1, ...), custom_call_target="tpu_custom_call" | custom-call | tf_op jit(solution)/shard_map/pallas_call | solution.py:484
  64.8 0.7 %copy.16 = bf16[128,1280]{1,0:T(8,128)(2,1)} copy(bf16[128,1280]{1,0:T(8,128)(2,1)S(1)} %get-tuple-element.6) | data formatting | bytes 655360
  65.5 0.7 %copy.17 = bf16[512,320]{0,1:T(8,128)(2,1)} copy(bf16[512,320]{0,1:T(8,128)(2,1)S(1)} %bitcast.5) | data formatting | bytes 655360

commit v4 on v3

--- a/solution.py
+++ b/solution.py
@@ -28,7 +28,7 @@
 def kernel(
     x_hbm, pos_hbm, g1_hbm, b1_hbm, wq_hbm, bq_hbm, wp_hbm, pb_hbm, g2_hbm, b2_hbm, fc_hbm, fb_hbm,
     vit_ref, hid_ref, x_ref, pos_ref, g1_ref, b1_ref, bq_ref, pb_ref, g2_ref, b2_ref, fb_ref,
-    gat, blk, wg, att, osend, qt, kk, vt, sc, fcv, wqv, bcol, fcol, zf,
+    gat, blk, wg, att, osend, qt, kk, vt, sc, fcv, wqv, bcol, fcol, zf, acc, osum, stat,
     ssend, srecv, precv, wsrecv, wprecv, asem, local,
 ):
     me = lax.axis_index("sp")
@@ -52,8 +52,9 @@
     loads = [pltpu.make_async_copy(src, dst, local.at[i]) for i, (src, dst) in enumerate(loads)]
     for load in loads:
         load.start()
-    for load in loads[:3]:
-        load.wait()
+    with jax.named_scope("s_load"):
+        for load in loads[:3]:
+            load.wait()
 
     ln_scope = jax.named_scope("s_ln")
     ln_scope.__enter__()
@@ -90,9 +91,16 @@
             self.copy((r, 0), (role, 0), 16, 16 * i, self.srecv.at[self.sem[role, i]], dx, dy, 0, other).start()
             self.rows += 16
 
+        def which(self, r, which):
+            return which if r in (5, 6, 7) else 0
+
+        def slot(self, r, which):
+            return 0 if self.precv is wprecv else (3 * (r - 5) + which - 1 + ROLES if which else r)
+
         def share(self, r, part):
             at, size, which = self.parts[part]
-            self.copy((r, 0), (r, 1), size, at, self.precv.at[r, which], 0, 0, 1).start()
+            which = self.which(r, which)
+            self.copy((r, 0), (r, 1), size, at, self.precv.at[self.slot(r, which)], 0, 0, 1).start()
             self.rows += size
 
         def wait(self, r, g):
@@ -108,9 +116,9 @@
             here.update(g)
 
         def wait_partner(self, r, which=0):
-            size = sum(v[1] for v in self.parts if v[2] == which)
-            at = min(v[0] for v in self.parts if v[2] == which)
-            self.copy((r, 1), (r, 1), size, at, self.precv.at[r, which], 0, 0, 1).wait_recv()
+            size = sum(v[1] for v in self.parts if self.which(r, v[2]) == which)
+            at = min(v[0] for v in self.parts if self.which(r, v[2]) == which)
+            self.copy((r, 1), (r, 1), size, at, self.precv.at[self.slot(r, which)], 0, 0, 1).wait_recv()
 
         def own(self, lo, hi):
             for a, b in list(zip(self.up + self.down, self.down + self.up))[lo:hi]:
@@ -166,7 +174,7 @@
             assert self.rows == 15 * size
             flat = self.ref.reshape(16 * size, D).at[pl.ds(0, self.rows)]
             pltpu.make_async_remote_copy(
-                src_ref=flat, dst_ref=flat, send_sem=self.ssend, recv_sem=self.precv.at[0, 0],
+                src_ref=flat, dst_ref=flat, send_sem=self.ssend, recv_sem=self.precv.at[0],
                 device_id={"sp": dev(0, 0, 1)}, device_id_type=MESH,
             ).wait_send()
 
@@ -198,15 +206,13 @@
             if i in (gw.up if r == 3 else gw.down):
                 gw.pass_on(r, i, 1 if r == 3 else -1, 0)
         for i in g:
-            if i in ((0, 1, 2) if r == 3 else (4, 3, 2)):
+            if i != (4 if r == 3 else 0):
                 gw.pass_on(r, i, 0, 1, r == 3)
 
     def w_cross():
         gw.wait(4, whole[0])
-        for i in (0, 1):
-            gw.pass_on(4, i, -1, 0)
-        for i in (4, 3):
-            gw.pass_on(4, i, 1, 0)
+        gw.pass_on(4, 0, -1, 0)
+        gw.pass_on(4, 4, 1, 0)
 
     def w_far(i):
         gw.wait(2, [i])
@@ -263,6 +269,49 @@
         qt[r, :, where] = jnp.concatenate([q, pad], axis=0).astype(jnp.bfloat16)
         kk[r, where] = jnp.concatenate([k, pad], axis=0).T.astype(jnp.bfloat16)
         vt[r, :, where] = v.astype(jnp.bfloat16)
+
+    early, late = (0, 3, 1, 4, 2), (5, 7, 6)
+
+    def score(r, slot, keys):
+        top = None
+        for n, c in enumerate(keys):
+            s = jnp.dot(kk[c], qt[r], preferred_element_type=jnp.float32)
+            sc[slot, n] = s
+            m = jnp.max(s.reshape(32, 8, 256), axis=0)
+            top = m if top is None else jnp.maximum(top, m)
+        return jnp.max(top, axis=0, keepdims=True) * SCALE
+
+    def weigh(slot, keys, top):
+        total, out = None, None
+        for n, c in enumerate(keys):
+            w = jnp.exp2(sc[slot, n] * SCALE - top)
+            s = jnp.sum(w.reshape(32, 8, 256), axis=0)
+            o = jnp.dot(vt[c], w.astype(jnp.bfloat16), preferred_element_type=jnp.float32)
+            total = s if total is None else total + s
+            out = o if out is None else out + o
+        return jnp.sum(total, axis=0, keepdims=True), out
+
+    def begin_tile(n, top):
+        later = score(early[n + 1], (n + 1) % 2, early) if n < 4 else None
+        total, out = weigh(n % 2, early, top)
+        osum[n] = out
+        stat[n, 0:1] = top
+        stat[n, 1:2] = total
+        return later
+
+    def end_tile(r, slot, top):
+        if r in early:
+            n = early.index(r)
+            before = stat[n, 0:1]
+            both = jnp.maximum(before, top)
+            total, out = weigh(slot, late, both)
+            old = jnp.exp2(before - both)
+            total, out = total + stat[n, 1:2] * old, out + osum[n] * old
+        else:
+            total, out = weigh(slot, early + late, top)
+        out = (out / total).astype(jnp.bfloat16)
+        for p in range(2):
+            osend[2 * r + p] = out[:, p * 128 : (p + 1) * 128]
 
     with jax.named_scope("a_own"):
         g1.wait_partner(0)
@@ -284,51 +333,44 @@
     with jax.named_scope("a_rest"):
         g1.rest()
     with jax.named_scope("a_qkv"):
-        for n, r in enumerate((3, 1, 4, 2)):
+        for r in (3, 1, 4, 2):
             g1.wait_partner(r)
             qkv(r)
-            if n > 0:
-                g1.last(pairs[n - 1])
+    with jax.named_scope("a_early0"):
+        top = score(early[0], 0, early)
+    with jax.named_scope("a_last0"):
+        g1.last(pairs[0])
+    with jax.named_scope("a_early1"):
+        top = begin_tile(0, top)
+        top = begin_tile(1, top)
+    with jax.named_scope("a_last1"):
+        g1.last(pairs[1])
+    with jax.named_scope("a_early2"):
+        top = begin_tile(2, top)
+        top = begin_tile(3, top)
+    with jax.named_scope("a_last2"):
+        g1.last(pairs[2])
+    with jax.named_scope("a_early3"):
+        begin_tile(4, top)
     with jax.named_scope("a_last"):
         g1.last(pairs[3])
+    with jax.named_scope("a_qkv2"):
+        for r in (5, 7, 6):
+            qkv(r, (0,))
     with jax.named_scope("w_ring0"):
         w_near(3, [0])
         w_near(1, [4])
-        w_cross()
-    with jax.named_scope("a_qkv2"):
-        for r in (5, 7, 6):
-            qkv(r, (0,))
-    with jax.named_scope("w_ring1"):
-        w_near(3, [1])
-        w_near(1, [3])
     with jax.named_scope("a_qkv3"):
-        for r in (5, 7, 6):
+        for n, r in enumerate((5, 7, 6)):
             g1.wait_partner(r)
             qkv(r, (1,))
-    with jax.named_scope("w_ring2"):
+            if n == 1:
+                w_near(3, [1])
+                w_near(1, [3])
+    with jax.named_scope("w_ring1"):
         w_near(3, [2])
         w_near(1, [2])
-
-    def score(r, slot):
-        top = None
-        for kc in range(ROLES):
-            s = jnp.dot(kk[kc], qt[r], preferred_element_type=jnp.float32)
-            sc[slot, kc] = s
-            m = jnp.max(s.reshape(32, 8, 256), axis=0)
-            top = m if top is None else jnp.maximum(top, m)
-        return jnp.max(top, axis=0, keepdims=True) * SCALE
-
-    def weigh(r, slot, top):
-        total, out = None, None
-        for kc in range(ROLES):
-            w = jnp.exp2(sc[slot, kc] * SCALE - top)
-            s = jnp.sum(w.reshape(32, 8, 256), axis=0)
-            o = jnp.dot(vt[kc], w.astype(jnp.bfloat16), preferred_element_type=jnp.float32)
-            total = s if total is None else total + s
-            out = o if out is None else out + o
-        out = (out / jnp.sum(total, axis=0, keepdims=True)).astype(jnp.bfloat16)
-        for p in range(2):
-            osend[2 * r + p] = out[:, p * 128 : (p + 1) * 128]
+        w_cross()
 
     def give(r):
         for p in range(2):
@@ -345,35 +387,40 @@
             ).start()
 
     order = (6, 7, 5, 2, 4, 3, 1, 0)
-    top = score(order[0], 0)
+    def keys(r):
+        return late if r in early else early + late
+
+    top = score(order[0], 0, keys(order[0]))
     for i, r in enumerate(order):
         if i + 1 < ROLES:
-            later = score(order[i + 1], (i + 1) % 2)
-        weigh(r, i % 2, top)
+            later = score(order[i + 1], (i + 1) % 2, keys(order[i + 1]))
+        end_tile(r, i % 2, top)
         top = later
         if i > 0:
             give(order[i - 1])
         with jax.named_scope(f"w_tile{i}"):
-            if i == 1:
+            if i == 0:
                 w_near(3, [3, 4])
                 w_near(1, [0, 1])
-            if i == 3:
+            if i == 2:
                 w_far(0)
                 w_far(4)
             if i == 4:
                 w_far(1)
                 w_far(3)
-            if i == 5:
-                w_far(2)
     with jax.named_scope("t_give"):
         give(order[-1])
         att[0] = osend[0]
+    with jax.named_scope("w_far"):
+        w_far(2)
     with jax.named_scope("w_last"):
         gw.last(two[0])
         gw.last(two[1])
     with jax.named_scope("w_partner"):
-        for r in range(ROLES):
-            gw.wait_partner(r)
+        pltpu.make_async_remote_copy(
+            src_ref=wg.at[:, 1], dst_ref=wg.at[:, 1], send_sem=ssend.at[2], recv_sem=wprecv.at[0],
+            device_id={"img": img, "sp": dev(0, 0, 1)}, device_id_type=MESH,
+        ).wait_recv()
     with jax.named_scope("t_back"):
         pltpu.make_async_remote_copy(
             src_ref=osend.at[pl.ds(1, 15)], dst_ref=att.at[pl.ds(1, 15)], send_sem=asem.at[0], recv_sem=asem.at[1],
@@ -439,30 +486,29 @@
         g2.last(pairs[0])
     with jax.named_scope("b_far_p"):
         for r in (0, 3, 1, 2, 4):
-            for j in range(4):
-                g2.wait_partner(r, j)
+            g2.wait_partner(r)
     with jax.named_scope("b_fc1_a"):
-        total = fc1(0, 0) + fc1(0, 1)
+        acc[...] = fc1(0, 0) + fc1(0, 1)
     with jax.named_scope("b_last1"):
         g2.last(pairs[1])
     with jax.named_scope("b_fc1_b"):
-        finish(0, total + fc1(0, 2) + fc1(0, 3))
+        finish(0, acc[...] + fc1(0, 2) + fc1(0, 3))
     partner(0)
     with jax.named_scope("b_fc1_c"):
-        total = fc1(1, 0)
+        acc[...] = fc1(1, 0)
+    partner(1)
+    with jax.named_scope("b_fc1_d"):
+        acc[...] += fc1(1, 1)
     with jax.named_scope("b_last2"):
         g2.last(pairs[2])
     with jax.named_scope("b_last3"):
         g2.last(pairs[3])
-    partner(1)
-    with jax.named_scope("b_fc1_d"):
-        total = total + fc1(1, 1)
     partner(2)
     with jax.named_scope("b_fc1_e"):
-        total = total + fc1(1, 2)
+        acc[...] += fc1(1, 2)
     partner(3)
     with jax.named_scope("b_fc1_f"):
-        finish(1, total + fc1(1, 3))
+        finish(1, acc[...] + fc1(1, 3))
 
     with jax.named_scope("drain"):
         for g in (g1, gw, g2):
@@ -471,6 +517,17 @@
             src_ref=osend.at[pl.ds(1, 15)], dst_ref=att.at[pl.ds(1, 15)], send_sem=asem.at[0], recv_sem=asem.at[1],
             device_id={"sp": dev(0, 0, 1)}, device_id_type=MESH,
         ).wait_send()
+
+
+def put(vit_ref, hid_ref, vit_hbm, hid_hbm, sem):
+    copies = [
+        pltpu.make_async_copy(vit_ref, vit_hbm, sem.at[0]),
+        pltpu.make_async_copy(hid_ref, hid_hbm, sem.at[1]),
+    ]
+    for copy in copies:
+        copy.start()
+    for copy in copies:
+        copy.wait()
 
 
 def per_device(
@@ -510,11 +567,14 @@
             pltpu.VMEM((3, HDIM, 128), f32),
             pltpu.VMEM((SHARE, 128), f32),
             pltpu.VMEM((D // 128, 128, 128), f32),
+            pltpu.VMEM((SHARE, 256), f32),
+            pltpu.VMEM((5, HDIM, 256), f32),
+            pltpu.VMEM((5, 8, 256), f32),
             dma((3,)),
             dma((35,)),
-            dma((ROLES, 4)),
+            dma((ROLES + 9,)),
             dma((20,)),
-            dma((ROLES, 1)),
+            dma((1,)),
             dma((2,)),
             dma((12,)),
         ],
@@ -535,6 +595,13 @@
         fc1_weight.T,
         fc1_bias,
     )
+    vit, hid = pl.pallas_call(
+        put,
+        out_shape=(jax.ShapeDtypeStruct((128, D), bf), jax.ShapeDtypeStruct((SHARE, 512), bf)),
+        in_specs=[vmem, vmem],
+        out_specs=(hbm, hbm),
+        scratch_shapes=[dma((2,))],
+    )(pltpu.with_memory_space_constraint(vit, pltpu.VMEM), pltpu.with_memory_space_constraint(hid, pltpu.VMEM))
     return vit, hid.T
 
 

time: 66.4 us -> 65 us (0.979)
  local copies, waits for them, and re-layouts: 1.45 us -> 0 us
    unnamed x2 -> x0, local copies, waits for them, and re-layouts: 1.45 us -> none
    pallas_call x0 -> x1, Pallas kernels: none -> 0.85 us  [per_device(): pl.pallas_call(put, out_shape=(jax.ShapeDtypeStruct((128, D), bf), jax.Sh...]
    pallas_call x1, Pallas kernels: 64.2 us -> 63.4 us  [per_device(): pl.pallas_call(kernel, out_shape=(pltpu.VMEM((128, D), bf), pltpu.VMEM((S...]
where the time goes in v4:
time: 65 us; the launch traced here: 64.9 us
  Pallas kernels  64.2 us (99%)
    pallas_call x1, Pallas kernels, per_device(): pl.pallas_call(kernel, out_shape=(pltpu.VMEM((128, D), bf), pltpu.VMEM((S...  63.4 us

profile of v4, /device:TPU:1, one launch (start us, length us, event | category | flops | bytes accessed | tf_op | source)
XLA Modules:
  0.0 64.9 jit_solution(10865477687169673750)
XLA Ops:
  0.6 63.4 %shard_map.131 = (bf16[128,1280]{1,0:T(8,128)(2,1)S(1)}, bf16[320,512]{1,0:T(8,128)(2,1)S(1)}) custom-call(bf16[128,1280]{1,0:T(8,128)(2,1)} %x_hbm.1, s32[2,2048]{1,0:T(2,128)} %pos_hbm.1, f32[1280]{0:T(1024)} %g1_hbm.1, f32[1280]{0:T(1024)} %b1_hbm.1, bf16[240,1280]{1,0:T(8,128)(2,1)} %bitcast.6, f32[3,1280]{1,0:T(4,128)} %bq_hbm.1, ...), custom_call_target="tpu_custom_call" | custom-call | tf_op jit(solution)/shard_map/pallas_call | solution.py:541
  64.0 0.9 %shard_map.132 = (bf16[128,1280]{1,0:T(8,128)(2,1)}, bf16[320,512]{1,0:T(8,128)(2,1)}) custom-call(bf16[128,1280]{1,0:T(8,128)(2,1)S(1)} %get-tuple-element.6.vit_ref, bf16[320,512]{1,0:T(8,128)(2,1)S(1)} %get-tuple-element.7.hid_ref), custom_call_target="tpu_custom_call" | custom-call | tf_op jit(solution)/shard_map/pallas_call | solution.py:598

commit v5 on v4

--- a/solution.py
+++ b/solution.py
@@ -29,7 +29,7 @@
     x_hbm, pos_hbm, g1_hbm, b1_hbm, wq_hbm, bq_hbm, wp_hbm, pb_hbm, g2_hbm, b2_hbm, fc_hbm, fb_hbm,
     vit_ref, hid_ref, x_ref, pos_ref, g1_ref, b1_ref, bq_ref, pb_ref, g2_ref, b2_ref, fb_ref,
     gat, blk, wg, att, osend, qt, kk, vt, sc, fcv, wqv, bcol, fcol, zf, acc, osum, stat,
-    ssend, srecv, precv, wsrecv, wprecv, asem, local,
+    wqo, trig, stage, kin, ssend, nrecv, nprecv, srecv, precv, wsrecv, wprecv, hsend, hrecv, asem, local,
 ):
     me = lax.axis_index("sp")
     img, images = lax.axis_index("img"), lax.axis_size("img")
@@ -46,8 +46,8 @@
     pl.semaphore_signal(barrier, inc=1, device_id={"img": (img + images // 2) % images, "sp": dev(0, 1, 0)}, device_id_type=MESH)
 
     loads = [
-        (x_hbm, x_ref), (g1_hbm, g1_ref), (b1_hbm, b1_ref), (wp_hbm, wg.at[0, 0]), (bq_hbm, bq_ref), (fb_hbm, fb_ref),
-        (wq_hbm, wqv), (pos_hbm, pos_ref), (pb_hbm, pb_ref), (g2_hbm, g2_ref), (b2_hbm, b2_ref), (fc_hbm, fcv),
+        (x_hbm, x_ref), (g1_hbm, g1_ref), (b1_hbm, b1_ref), (wq_hbm, wqv), (wp_hbm, wg.at[0, 0]), (bq_hbm, bq_ref),
+        (fb_hbm, fb_ref), (pos_hbm, pos_ref), (pb_hbm, pb_ref), (g2_hbm, g2_ref), (b2_hbm, b2_ref), (fc_hbm, fcv),
     ]
     loads = [pltpu.make_async_copy(src, dst, local.at[i]) for i, (src, dst) in enumerate(loads)]
     for load in loads:
@@ -71,7 +71,7 @@
             self.ref, self.up, self.down, self.across, self.flow = ref, up, down, across, flow
             self.groups, self.parts, self.srecv, self.precv, self.ssend = groups, parts, srecv, precv, ssend
             self.rows, self.here, self.sem = 0, {}, {}
-            for r in range(1, ROLES):
+            for r in sorted(groups):
                 for g in groups[r]:
                     for i in g:
                         self.sem[r, i] = len(set(self.sem.values())) if i == g[0] else self.sem[r, g[0]]
@@ -144,9 +144,10 @@
                 if n in (1, 3):
                     self.own(6 + n // 2, 7 + n // 2)
 
-        def ring(self, r, i):
-            self.wait(r, [i])
-            self.pass_on(r, i, 1 if r == 3 else -1, 0)
+        def ring(self, r, *g):
+            self.wait(r, list(g))
+            for i in g:
+                self.pass_on(r, i, 1 if r == 3 else -1, 0)
 
         def cross(self, g):
             self.wait(4, g)
@@ -170,9 +171,9 @@
                 self.wait(r, g)
 
         def drain(self):
-            size = self.ref.shape[2]
-            assert self.rows == 15 * size
-            flat = self.ref.reshape(16 * size, D).at[pl.ds(0, self.rows)]
+            total = self.ref.shape[0] * self.ref.shape[1] * self.ref.shape[2]
+            assert self.rows <= total
+            flat = self.ref.reshape(total, D).at[pl.ds(0, self.rows)]
             pltpu.make_async_remote_copy(
                 src_ref=flat, dst_ref=flat, send_sem=self.ssend, recv_sem=self.precv.at[0],
                 device_id={"sp": dev(0, 0, 1)}, device_id_type=MESH,
@@ -188,7 +189,15 @@
     }
     flow = [0, 2, 1, 3, 4, 6, 5, 7]
     big = ([0, 1, 4, 5], [2, 3, 6, 7], 7, flow, groups)
-    g1 = Gather(gat, *big, [(32 * j, 32, 0) for j in range(4)], srecv, precv, ssend.at[0])
+    row_groups = {
+        1: [[2, 3], [6, 7], [0, 1], [4, 5]],
+        2: [[0, 1], [2, 3], [4, 5], [6, 7]],
+        3: [[0, 1], [4, 5], [2, 3], [6, 7]],
+    }
+    g1 = Gather(
+        gat, [0, 1, 4, 5], [2, 3, 6, 7], None, None, row_groups, [(32 * j, 32, 0) for j in range(4)], nrecv, nprecv,
+        ssend.at[0],
+    )
     g2 = Gather(blk, *big, [(32 * j, 32, j) for j in range(4)], srecv, precv, ssend.at[1])
     whole = [[0, 1, 2, 3, 4]]
     two = [[0, 1, 2], [3, 4]]
@@ -206,71 +215,104 @@
             if i in (gw.up if r == 3 else gw.down):
                 gw.pass_on(r, i, 1 if r == 3 else -1, 0)
         for i in g:
-            if i != (4 if r == 3 else 0):
-                gw.pass_on(r, i, 0, 1, r == 3)
+            if r == 3 and i != 4:
+                gw.pass_on(r, i, 0, 1, True)
 
     def w_cross():
         gw.wait(4, whole[0])
-        gw.pass_on(4, 0, -1, 0)
         gw.pass_on(4, 4, 1, 0)
+        for i in (4, 3, 2, 1, 0):
+            gw.pass_on(4, i, -1, 0)
 
     def w_far(i):
         gw.wait(2, [i])
-        gw.pass_on(2, i, 0, 1, i != 0)
-
-    g1.begin()
+        gw.pass_on(2, i, 0, 1, True)
+
+    def head_weights(at, size, sem, other=False):
+        return pltpu.make_async_remote_copy(
+            src_ref=wqv.at[pl.ds(at, size)], dst_ref=wqo.at[pl.ds(at, size)], send_sem=hsend.at[0], recv_sem=hrecv.at[sem],
+            device_id={"img": (img + images // 2) % images if other else img, "sp": dev(0, 1, 0)}, device_id_type=MESH,
+        )
+
+    g1.own(0, 8)
     loads[3].wait()
+    for i in range(15):
+        head_weights(16 * i, 16, 0 if i < 10 else 1, i % 2 == 0).start()
+    loads[4].wait()
     for i in range(5):
         gw.pass_on(0, i, 0, 1, True)
+    g1.share_own()
     gw.share_own()
 
-    for load in loads[4:6]:
+    for load in loads[5:8]:
         load.wait()
     lane = lax.broadcasted_iota(jnp.int32, (HDIM, D), 1)
     sub = lax.broadcasted_iota(jnp.int32, (HDIM, D), 0)
-    mine = lane == sub + me * HDIM
-    for c in range(3):
-        col = jnp.sum(jnp.where(mine, bq_ref[c : c + 1, :], 0.0), axis=1, keepdims=True)
-        bcol[c] = jnp.broadcast_to(col, (HDIM, 128))
+    for n, head in enumerate((me, dev(0, 1, 0))):
+        mine = lane == sub + head * HDIM
+        for c in range(3):
+            col = jnp.sum(jnp.where(mine, bq_ref[c : c + 1, :], 0.0), axis=1, keepdims=True)
+            bcol[3 * n + c] = jnp.broadcast_to(col, (HDIM, 128))
     same = lax.broadcasted_iota(jnp.int32, (SHARE, SHARE), 0) == lax.broadcasted_iota(
         jnp.int32, (SHARE, SHARE), 1
     )
     col = jnp.sum(jnp.where(same, fb_ref[...].reshape(1, SHARE), 0.0), axis=1, keepdims=True)
     fcol[...] = jnp.broadcast_to(col, (SHARE, 128))
-
-    for load in loads[6:8]:
-        load.wait()
-
-    def qkv(r, ps=(0, 1)):
-        n = 128 * len(ps)
-        rows = gat[r, ps[0] : ps[-1] + 1].reshape(n, D)
-        out = lax.dot_general(
-            wqv[...], rows, (((1,), (1,)), ((), ())), preferred_element_type=jnp.float32
-        )
-        at = [pl.multiple_of(dev(r % 4, r // 4, p) * 128, 128) for p in ps]
+    for r in range(4):
+        at = [pl.multiple_of(dev(r, 0, p) * 128, 128) for p in range(2)]
         prow = jnp.concatenate([pos_ref[0:1, pl.ds(a, 128)] for a in at], axis=1).astype(jnp.float32)
         pcol = jnp.concatenate([pos_ref[1:2, pl.ds(a, 128)] for a in at], axis=1).astype(jnp.float32)
-        row = lax.broadcasted_iota(jnp.int32, (40, n), 0)
+        row = lax.broadcasted_iota(jnp.int32, (40, 256), 0)
         power = jnp.where(row < 20, row, row - 20).astype(jnp.float32)
         inv = jnp.exp2(power * (-math.log2(10000.0) / 20.0))
         angle = jnp.where(row < 20, prow, pcol) * inv
-        cos, sin = jnp.cos(angle), jnp.sin(angle)
-
-        def turn(v):
-            lo, hi = v[:40], v[40:]
-            return jnp.concatenate([lo * cos - hi * sin, hi * cos + lo * sin], axis=0)
-
-        bias = [jnp.concatenate([bcol[c]] * len(ps), axis=1) for c in range(3)]
-        pad = jnp.zeros((128 - HDIM, n), jnp.float32)
-        q = turn(out[0:80] + bias[0])
-        k = turn(out[80:160] + bias[1])
-        v = out[160:240] + bias[2]
-        where = pl.ds(ps[0] * 128, n)
-        qt[r, :, where] = jnp.concatenate([q, pad], axis=0).astype(jnp.bfloat16)
-        kk[r, where] = jnp.concatenate([k, pad], axis=0).T.astype(jnp.bfloat16)
-        vt[r, :, where] = v.astype(jnp.bfloat16)
-
-    early, late = (0, 3, 1, 4, 2), (5, 7, 6)
+        trig[r, 0] = jnp.cos(angle)
+        trig[r, 1] = jnp.sin(angle)
+    for r in range(4, ROLES):
+        qt[r, HDIM:128] = jnp.zeros((128 - HDIM, 256), jnp.bfloat16)
+
+    def project(weights, r, ps):
+        rows = gat[r, ps[0] : ps[-1] + 1].reshape(128 * len(ps), D)
+        return lax.dot_general(weights, rows, (((1,), (1,)), ((), ())), preferred_element_type=jnp.float32)
+
+    def finish_head(v, r, ps, n, c):
+        v = v + jnp.concatenate([bcol[3 * n + c]] * len(ps), axis=1)
+        if c == 2:
+            return v
+        cos, sin = (trig[r, t, :, pl.ds(128 * ps[0], 128 * len(ps))] for t in range(2))
+        lo, hi = v[:40], v[40:]
+        return jnp.concatenate([lo * cos - hi * sin, hi * cos + lo * sin], axis=0)
+
+    def turned_keys(k):
+        return jnp.concatenate([k, jnp.zeros((128 - HDIM, 256), jnp.float32)], axis=0).T.astype(jnp.bfloat16)
+
+    def qkv(r):
+        out = project(wqv[...], r, (0, 1))
+        q, k, v = (finish_head(out[80 * c : 80 * c + 80], r, (0, 1), 0, c) for c in range(3))
+        qt[r] = jnp.concatenate([q, jnp.zeros((128 - HDIM, 256), jnp.float32)], axis=0).astype(jnp.bfloat16)
+        kk[r] = turned_keys(k)
+        vt[r] = v.astype(jnp.bfloat16)
+
+    def qkv_other(r, ps, cs=(0, 1, 2)):
+        out = project(wqo[80 * cs[0] : 80 * cs[-1] + 80], r, ps)
+        lanes = pl.ds(128 * ps[0], 128 * len(ps))
+        for n, c in enumerate(cs):
+            stage[r, c, :, lanes] = finish_head(out[80 * n : 80 * n + 80], r, ps, 1, c).astype(jnp.bfloat16)
+        for c in cs:
+            dst = (qt.at[4 + r, pl.ds(0, HDIM), lanes], kin.at[r, :, lanes], vt.at[4 + r, :, lanes])[c]
+            pltpu.make_async_remote_copy(
+                src_ref=stage.at[r, c, :, lanes], dst_ref=dst, send_sem=hsend.at[1], recv_sem=hrecv.at[2 + r],
+                device_id={"img": img, "sp": dev(0, 1, 0)}, device_id_type=MESH,
+            ).start()
+
+    def receive(r):
+        pltpu.make_async_remote_copy(
+            src_ref=stage.at[r], dst_ref=stage.at[r], send_sem=hsend.at[1], recv_sem=hrecv.at[2 + r],
+            device_id={"img": img, "sp": dev(0, 1, 0)}, device_id_type=MESH,
+        ).wait_recv()
+        kk[4 + r] = turned_keys(kin[r].astype(jnp.float32))
+
+    early, late = (0, 3, 1, 2, 4), (7, 5, 6)
 
     def score(r, slot, keys):
         top = None
@@ -317,60 +359,76 @@
         g1.wait_partner(0)
         qkv(0)
     with jax.named_scope("a_ring"):
-        g1.ring_all()
-    with jax.named_scope("a_cross"):
-        g1.cross(halves[0])
-    with jax.named_scope("a_far0"):
-        for i in flow[:4]:
-            g1.far(i)
-    with jax.named_scope("a_cross1"):
-        g1.cross(halves[1])
-    with jax.named_scope("a_far1"):
-        for i in flow[4:]:
-            g1.far(i)
-    with jax.named_scope("a_wbegin"):
+        g1.ring(3, 0, 1)
+        g1.ring(1, 2, 3)
+        g1.ring(3, 4, 5)
+        g1.ring(1, 6, 7)
         gw.own(0, 5)
+    with jax.named_scope("a_other0"):
+        head_weights(0, 160, 0).wait_recv()
+        qkv_other(0, (0, 1), (0, 1))
     with jax.named_scope("a_rest"):
-        g1.rest()
-    with jax.named_scope("a_qkv"):
-        for r in (3, 1, 4, 2):
+        for r in (3, 1):
+            g1.wait(r, row_groups[r][2])
+            g1.wait(r, row_groups[r][3])
+    with jax.named_scope("a_other0v"):
+        head_weights(160, 80, 1).wait_recv()
+        qkv_other(0, (0, 1), (2,))
+    with jax.named_scope("a_near"):
+        for r in (3, 1):
+            qkv_other(r, (0,))
+    with jax.named_scope("a_near_p"):
+        for r in (3, 1):
             g1.wait_partner(r)
-            qkv(r)
+            qkv_other(r, (1,))
+    with jax.named_scope("a_near_own"):
+        qkv(3)
+        qkv(1)
+    with jax.named_scope("a_two"):
+        for g in row_groups[2]:
+            g1.wait(2, g)
+        qkv_other(2, (0,))
+    with jax.named_scope("w_ring0"):
+        w_near(3, [0])
+        w_near(1, [4])
+    with jax.named_scope("a_two_p"):
+        g1.wait_partner(2)
+        qkv_other(2, (1,))
+        qkv(2)
+    with jax.named_scope("w_ring1"):
+        w_near(3, [1])
+        w_near(1, [3])
+    with jax.named_scope("a_recv0"):
+        receive(0)
     with jax.named_scope("a_early0"):
         top = score(early[0], 0, early)
-    with jax.named_scope("a_last0"):
-        g1.last(pairs[0])
+        top = begin_tile(0, top)
+    with jax.named_scope("w_ring2"):
+        w_near(3, [2])
+        w_near(1, [2])
+        w_cross()
     with jax.named_scope("a_early1"):
-        top = begin_tile(0, top)
         top = begin_tile(1, top)
-    with jax.named_scope("a_last1"):
-        g1.last(pairs[1])
+    with jax.named_scope("w_ring3"):
+        w_near(3, [3, 4])
+        w_near(1, [0, 1])
+    with jax.named_scope("a_recv3"):
+        receive(3)
     with jax.named_scope("a_early2"):
         top = begin_tile(2, top)
         top = begin_tile(3, top)
-    with jax.named_scope("a_last2"):
-        g1.last(pairs[2])
+    with jax.named_scope("w_far0"):
+        w_far(0)
+        w_far(4)
+    with jax.named_scope("a_recv1"):
+        receive(1)
     with jax.named_scope("a_early3"):
         begin_tile(4, top)
-    with jax.named_scope("a_last"):
-        g1.last(pairs[3])
-    with jax.named_scope("a_qkv2"):
-        for r in (5, 7, 6):
-            qkv(r, (0,))
-    with jax.named_scope("w_ring0"):
-        w_near(3, [0])
-        w_near(1, [4])
-    with jax.named_scope("a_qkv3"):
-        for n, r in enumerate((5, 7, 6)):
-            g1.wait_partner(r)
-            qkv(r, (1,))
-            if n == 1:
-                w_near(3, [1])
-                w_near(1, [3])
-    with jax.named_scope("w_ring1"):
-        w_near(3, [2])
-        w_near(1, [2])
-        w_cross()
+    with jax.named_scope("w_far1"):
+        w_far(1)
+        w_far(3)
+    with jax.named_scope("a_recv2"):
+        receive(2)
 
     def give(r):
         for p in range(2):
@@ -398,21 +456,12 @@
         top = later
         if i > 0:
             give(order[i - 1])
-        with jax.named_scope(f"w_tile{i}"):
-            if i == 0:
-                w_near(3, [3, 4])
-                w_near(1, [0, 1])
-            if i == 2:
-                w_far(0)
-                w_far(4)
-            if i == 4:
-                w_far(1)
-                w_far(3)
+        if i == 0:
+            with jax.named_scope("w_far2"):
+                w_far(2)
     with jax.named_scope("t_give"):
         give(order[-1])
         att[0] = osend[0]
-    with jax.named_scope("w_far"):
-        w_far(2)
     with jax.named_scope("w_last"):
         gw.last(two[0])
         gw.last(two[1])
@@ -513,6 +562,11 @@
     with jax.named_scope("drain"):
         for g in (g1, gw, g2):
             g.drain()
+        head_weights(0, 3 * HDIM, 0).wait_send()
+        pltpu.make_async_remote_copy(
+            src_ref=stage, dst_ref=stage, send_sem=hsend.at[1], recv_sem=hrecv.at[2],
+            device_id={"img": img, "sp": dev(0, 1, 0)}, device_id_type=MESH,
+        ).wait_send()
         pltpu.make_async_remote_copy(
             src_ref=osend.at[pl.ds(1, 15)], dst_ref=att.at[pl.ds(1, 15)], send_sem=asem.at[0], recv_sem=asem.at[1],
             device_id={"sp": dev(0, 0, 1)}, device_id_type=MESH,
@@ -553,7 +607,7 @@
             pltpu.VMEM((D,), f32),
             pltpu.VMEM((D,), f32),
             pltpu.VMEM((SHARE,), f32),
-            pltpu.VMEM((ROLES, 2, 128, D), bf),
+            pltpu.VMEM((4, 2, 128, D), bf),
             pltpu.VMEM((ROLES, 2, 128, D), bf),
             pltpu.VMEM((ROLES, 2, HDIM, D), bf),
             pltpu.VMEM((2 * ROLES, HDIM, 128), bf),
@@ -564,17 +618,25 @@
             pltpu.VMEM((2, ROLES, 256, 256), f32),
             pltpu.VMEM((SHARE, HIDDEN), bf),
             pltpu.VMEM((3 * HDIM, D), bf),
-            pltpu.VMEM((3, HDIM, 128), f32),
+            pltpu.VMEM((6, HDIM, 128), f32),
             pltpu.VMEM((SHARE, 128), f32),
             pltpu.VMEM((D // 128, 128, 128), f32),
             pltpu.VMEM((SHARE, 256), f32),
             pltpu.VMEM((5, HDIM, 256), f32),
             pltpu.VMEM((5, 8, 256), f32),
+            pltpu.VMEM((3 * HDIM, D), bf),
+            pltpu.VMEM((4, 2, 40, 256), f32),
+            pltpu.VMEM((4, 3, HDIM, 256), bf),
+            pltpu.VMEM((4, HDIM, 256), bf),
             dma((3,)),
+            dma((12,)),
+            dma((4,)),
             dma((35,)),
             dma((ROLES + 9,)),
             dma((20,)),
             dma((1,)),
+            dma((2,)),
+            dma((6,)),
             dma((2,)),
             dma((12,)),
         ],

time: 65 us -> 61.4 us (0.945)
  Pallas kernels: 64.2 us -> 60.5 us
    pallas_call x1, Pallas kernels: 63.4 us -> 59.6 us  [per_device(): pl.pallas_call(kernel, out_shape=(pltpu.VMEM((128, D), bf), pltpu.VMEM((S...]
where the time goes in v5:
time: 61.4 us; the launch traced here: 61.3 us
  Pallas kernels  60.5 us (99%)
  between operations  0.8 us (1%)
    pallas_call x1, Pallas kernels, per_device(): pl.pallas_call(kernel, out_shape=(pltpu.VMEM((128, D), bf), pltpu.VMEM((S...  59.6 us

profile of v5, /device:TPU:1, one launch (start us, length us, event | category | flops | bytes accessed | tf_op | source)
XLA Modules:
  0.0 61.3 jit_solution(9094912569132401863)
XLA Ops:
  0.6 59.6 %shard_map.131 = (bf16[128,1280]{1,0:T(8,128)(2,1)S(1)}, bf16[320,512]{1,0:T(8,128)(2,1)S(1)}) custom-call(bf16[128,1280]{1,0:T(8,128)(2,1)} %x_hbm.1, s32[2,2048]{1,0:T(2,128)} %pos_hbm.1, f32[1280]{0:T(1024)} %g1_hbm.1, f32[1280]{0:T(1024)} %b1_hbm.1, bf16[240,1280]{1,0:T(8,128)(2,1)} %bitcast.6, f32[3,1280]{1,0:T(4,128)} %bq_hbm.1, ...), custom_call_target="tpu_custom_call" | custom-call | tf_op jit(solution)/shard_map/pallas_call | solution.py:595
  60.2 0.9 %shard_map.132 = (bf16[128,1280]{1,0:T(8,128)(2,1)}, bf16[320,512]{1,0:T(8,128)(2,1)}) custom-call(bf16[128,1280]{1,0:T(8,128)(2,1)S(1)} %get-tuple-element.6.vit_ref, bf16[320,512]{1,0:T(8,128)(2,1)S(1)} %get-tuple-element.7.hid_ref), custom_call_target="tpu_custom_call" | custom-call | tf_op jit(solution)/shard_map/pallas_call | solution.py:660

commit v6 on v5

--- a/solution.py
+++ b/solution.py
@@ -29,7 +29,7 @@
     x_hbm, pos_hbm, g1_hbm, b1_hbm, wq_hbm, bq_hbm, wp_hbm, pb_hbm, g2_hbm, b2_hbm, fc_hbm, fb_hbm,
     vit_ref, hid_ref, x_ref, pos_ref, g1_ref, b1_ref, bq_ref, pb_ref, g2_ref, b2_ref, fb_ref,
     gat, blk, wg, att, osend, qt, kk, vt, sc, fcv, wqv, bcol, fcol, zf, acc, osum, stat,
-    wqo, trig, stage, kin, ssend, nrecv, nprecv, srecv, precv, wsrecv, wprecv, hsend, hrecv, asem, local,
+    wqo, trig, stage, kin, ssend, srecv, precv, wsrecv, wprecv, hsend, hrecv, asem, local,
 ):
     me = lax.axis_index("sp")
     img, images = lax.axis_index("img"), lax.axis_size("img")
@@ -195,7 +195,7 @@
         3: [[0, 1], [4, 5], [2, 3], [6, 7]],
     }
     g1 = Gather(
-        gat, [0, 1, 4, 5], [2, 3, 6, 7], None, None, row_groups, [(32 * j, 32, 0) for j in range(4)], nrecv, nprecv,
+        gat, [0, 1, 4, 5], [2, 3, 6, 7], None, None, row_groups, [(32 * j, 32, 0) for j in range(4)], srecv, precv,
         ssend.at[0],
     )
     g2 = Gather(blk, *big, [(32 * j, 32, j) for j in range(4)], srecv, precv, ssend.at[1])
@@ -221,7 +221,7 @@
     def w_cross():
         gw.wait(4, whole[0])
         gw.pass_on(4, 4, 1, 0)
-        for i in (4, 3, 2, 1, 0):
+        for i in range(5):
             gw.pass_on(4, i, -1, 0)
 
     def w_far(i):
@@ -312,7 +312,7 @@
         ).wait_recv()
         kk[4 + r] = turned_keys(kin[r].astype(jnp.float32))
 
-    early, late = (0, 3, 1, 2, 4), (7, 5, 6)
+    early, late, ahead = (0, 3, 1, 2, 4), (7, 5, 6), (0, 3, 1, 2, 4, 7, 5)
 
     def score(r, slot, keys):
         top = None
@@ -333,8 +333,8 @@
             out = o if out is None else out + o
         return jnp.sum(total, axis=0, keepdims=True), out
 
-    def begin_tile(n, top):
-        later = score(early[n + 1], (n + 1) % 2, early) if n < 4 else None
+    def begin_tile(n, top, more=True):
+        later = score(ahead[n + 1], (n + 1) % 2, early) if more else None
         total, out = weigh(n % 2, early, top)
         osum[n] = out
         stat[n, 0:1] = top
@@ -342,8 +342,8 @@
         return later
 
     def end_tile(r, slot, top):
-        if r in early:
-            n = early.index(r)
+        if r in ahead:
+            n = ahead.index(r)
             before = stat[n, 0:1]
             both = jnp.maximum(before, top)
             total, out = weigh(slot, late, both)
@@ -398,6 +398,7 @@
     with jax.named_scope("w_ring1"):
         w_near(3, [1])
         w_near(1, [3])
+        w_cross()
     with jax.named_scope("a_recv0"):
         receive(0)
     with jax.named_scope("a_early0"):
@@ -406,27 +407,31 @@
     with jax.named_scope("w_ring2"):
         w_near(3, [2])
         w_near(1, [2])
-        w_cross()
     with jax.named_scope("a_early1"):
         top = begin_tile(1, top)
+        top = begin_tile(2, top)
     with jax.named_scope("w_ring3"):
         w_near(3, [3, 4])
         w_near(1, [0, 1])
+    with jax.named_scope("a_early2"):
+        top = begin_tile(3, top)
     with jax.named_scope("a_recv3"):
         receive(3)
-    with jax.named_scope("a_early2"):
-        top = begin_tile(2, top)
-        top = begin_tile(3, top)
     with jax.named_scope("w_far0"):
         w_far(0)
         w_far(4)
+    with jax.named_scope("a_early3"):
+        top = begin_tile(4, top)
     with jax.named_scope("a_recv1"):
         receive(1)
-    with jax.named_scope("a_early3"):
-        begin_tile(4, top)
     with jax.named_scope("w_far1"):
         w_far(1)
         w_far(3)
+    with jax.named_scope("a_early4"):
+        top = begin_tile(5, top)
+        begin_tile(6, top, False)
+    with jax.named_scope("w_far2"):
+        w_far(2)
     with jax.named_scope("a_recv2"):
         receive(2)
 
@@ -446,7 +451,7 @@
 
     order = (6, 7, 5, 2, 4, 3, 1, 0)
     def keys(r):
-        return late if r in early else early + late
+        return late if r in ahead else early + late
 
     top = score(order[0], 0, keys(order[0]))
     for i, r in enumerate(order):
@@ -456,15 +461,18 @@
         top = later
         if i > 0:
             give(order[i - 1])
-        if i == 0:
-            with jax.named_scope("w_far2"):
-                w_far(2)
+        if i == 4:
+            with jax.named_scope("w_last0"):
+                gw.wait(7, two[0])
+                gw.wait(5, two[0])
     with jax.named_scope("t_give"):
         give(order[-1])
         att[0] = osend[0]
     with jax.named_scope("w_last"):
-        gw.last(two[0])
-        gw.last(two[1])
+        gw.wait(6, two[1])
+        gw.wait(5, two[1])
+        gw.wait(7, two[1])
+        gw.wait(6, two[0])
     with jax.named_scope("w_partner"):
         pltpu.make_async_remote_copy(
             src_ref=wg.at[:, 1], dst_ref=wg.at[:, 1], send_sem=ssend.at[2], recv_sem=wprecv.at[0],
@@ -542,16 +550,16 @@
         g2.last(pairs[1])
     with jax.named_scope("b_fc1_b"):
         finish(0, acc[...] + fc1(0, 2) + fc1(0, 3))
+    with jax.named_scope("b_last2"):
+        g2.last(pairs[2])
     partner(0)
     with jax.named_scope("b_fc1_c"):
         acc[...] = fc1(1, 0)
+    with jax.named_scope("b_last3"):
+        g2.last(pairs[3])
     partner(1)
     with jax.named_scope("b_fc1_d"):
         acc[...] += fc1(1, 1)
-    with jax.named_scope("b_last2"):
-        g2.last(pairs[2])
-    with jax.named_scope("b_last3"):
-        g2.last(pairs[3])
     partner(2)
     with jax.named_scope("b_fc1_e"):
         acc[...] += fc1(1, 2)
@@ -622,15 +630,13 @@
             pltpu.VMEM((SHARE, 128), f32),
             pltpu.VMEM((D // 128, 128, 128), f32),
             pltpu.VMEM((SHARE, 256), f32),
-            pltpu.VMEM((5, HDIM, 256), f32),
-            pltpu.VMEM((5, 8, 256), f32),
+            pltpu.VMEM((7, HDIM, 256), f32),
+            pltpu.VMEM((7, 8, 256), f32),
             pltpu.VMEM((3 * HDIM, D), bf),
             pltpu.VMEM((4, 2, 40, 256), f32),
             pltpu.VMEM((4, 3, HDIM, 256), bf),
             pltpu.VMEM((4, HDIM, 256), bf),
             dma((3,)),
-            dma((12,)),
-            dma((4,)),
             dma((35,)),
             dma((ROLES + 9,)),
             dma((20,)),

time: 61.4 us -> 60.7 us (0.989)
  no operation moved by 1% of the time
where the time goes in v6:
time: 60.7 us; the launch traced here: 60.6 us
  Pallas kernels  60 us (99%)
  between operations  0.64 us (1%)
    pallas_call x1, Pallas kernels, per_device(): pl.pallas_call(kernel, out_shape=(pltpu.VMEM((128, D), bf), pltpu.VMEM((S...  59.1 us

profile of v6, /device:TPU:1, one launch (start us, length us, event | category | flops | bytes accessed | tf_op | source)
XLA Modules:
  0.0 60.6 jit_solution(8975293360345250101)
XLA Ops:
  0.6 59.1 %shard_map.131 = (bf16[128,1280]{1,0:T(8,128)(2,1)S(1)}, bf16[320,512]{1,0:T(8,128)(2,1)S(1)}) custom-call(bf16[128,1280]{1,0:T(8,128)(2,1)} %x_hbm.1, s32[2,2048]{1,0:T(2,128)} %pos_hbm.1, f32[1280]{0:T(1024)} %g1_hbm.1, f32[1280]{0:T(1024)} %b1_hbm.1, bf16[240,1280]{1,0:T(8,128)(2,1)} %bitcast.6, f32[3,1280]{1,0:T(4,128)} %bq_hbm.1, ...), custom_call_target="tpu_custom_call" | custom-call | tf_op jit(solution)/shard_map/pallas_call | solution.py:603
  59.8 0.9 %shard_map.132 = (bf16[128,1280]{1,0:T(8,128)(2,1)}, bf16[320,512]{1,0:T(8,128)(2,1)}) custom-call(bf16[128,1280]{1,0:T(8,128)(2,1)S(1)} %get-tuple-element.6.vit_ref, bf16[320,512]{1,0:T(8,128)(2,1)S(1)} %get-tuple-element.7.hid_ref), custom_call_target="tpu_custom_call" | custom-call | tf_op jit(solution)/shard_map/pallas_call | solution.py:666

commit v7 on v6

--- a/solution.py
+++ b/solution.py
@@ -449,7 +449,7 @@
                 device_id_type=MESH,
             ).start()
 
-    order = (6, 7, 5, 2, 4, 3, 1, 0)
+    order = (2, 7, 6, 5, 4, 3, 1, 0)
     def keys(r):
         return late if r in ahead else early + late
 

time: 60.7 us -> 60.8 us (level)
  no operation moved by 1% of the time
where the time goes in v7:
time: 60.8 us; the launch traced here: 60.7 us
  Pallas kernels  60.1 us (99%)
  between operations  0.64 us (1%)
    pallas_call x1, Pallas kernels, per_device(): pl.pallas_call(kernel, out_shape=(pltpu.VMEM((128, D), bf), pltpu.VMEM((S...  59.2 us

profile of v7, /device:TPU:1, one launch (start us, length us, event | category | flops | bytes accessed | tf_op | source)
XLA Modules:
  0.0 60.7 jit_solution(14100838291556684378)
XLA Ops:
  0.6 59.2 %shard_map.131 = (bf16[128,1280]{1,0:T(8,128)(2,1)S(1)}, bf16[320,512]{1,0:T(8,128)(2,1)S(1)}) custom-call(bf16[128,1280]{1,0:T(8,128)(2,1)} %x_hbm.1, s32[2,2048]{1,0:T(2,128)} %pos_hbm.1, f32[1280]{0:T(1024)} %g1_hbm.1, f32[1280]{0:T(1024)} %b1_hbm.1, bf16[240,1280]{1,0:T(8,128)(2,1)} %bitcast.6, f32[3,1280]{1,0:T(4,128)} %bq_hbm.1, ...), custom_call_target="tpu_custom_call" | custom-call | tf_op jit(solution)/shard_map/pallas_call | solution.py:603
  59.8 0.9 %shard_map.132 = (bf16[128,1280]{1,0:T(8,128)(2,1)}, bf16[320,512]{1,0:T(8,128)(2,1)}) custom-call(bf16[128,1280]{1,0:T(8,128)(2,1)S(1)} %get-tuple-element.6.vit_ref, bf16[320,512]{1,0:T(8,128)(2,1)S(1)} %get-tuple-element.7.hid_ref), custom_call_target="tpu_custom_call" | custom-call | tf_op jit(solution)/shard_map/pallas_call | solution.py:666
